TPU v7x, 8 devices: a whole 2x2x1 slice. The times are simulated.
8 devices in a mesh: dp: 1 (over z), cp: 8 (over y, x, core).
Axes of the slice: x: 2, y: 2, z: 1, core: 2. Of those that a mesh axis runs over, the one named last changes fastest.
Arguments:
- queries: bfloat16 [3, 3072, 32, 128], P('dp', 'cp')
- keys: bfloat16 [3, 3072, 16, 128], P('dp', 'cp')
- values: bfloat16 [3, 3072, 16, 128], P('dp', 'cp')
- out_grad: bfloat16 [3, 3072, 32, 128], P('dp', 'cp')
Outputs:
- output 1: bfloat16 [3, 3072, 32, 128], P('dp', 'cp')
- output 2: float32 [3, 32, 3072], P('dp', None, 'cp')
- output 3: bfloat16 [3, 3072, 32, 128], P('dp', 'cp')
- output 4: bfloat16 [3, 3072, 16, 128], P('dp', 'cp')
- output 5: bfloat16 [3, 3072, 16, 128], P('dp', 'cp')
All inputs are finite; a program needn't handle non-finite values.
Results may differ from a plain program's by a relative error of at most 0.0187816.
Values are sent between devices in bfloat16 or wider.
A program may use at most 1 GiB of HBM per device.

v0:
```python
import jax
import jax.numpy as jnp
from jax import lax
from jax.sharding import PartitionSpec as P


def block_scores(query5, key_blk, scale, causal):
    scores = jnp.einsum("bqgrd,bkgd->bgrqk", query5, key_blk, preferred_element_type=jnp.float32) * scale
    if causal:
        tokens = query5.shape[1]
        row_idx = lax.broadcasted_iota(jnp.int32, (tokens, tokens), 0)
        col_idx = lax.broadcasted_iota(jnp.int32, (tokens, tokens), 1)
        scores = jnp.where(row_idx >= col_idx, scores, -jnp.inf)
    return scores


def forward_step(query5, key_blk, value_blk, state, scale, causal):
    run_max, run_sum, run_acc = state
    scores = block_scores(query5, key_blk, scale, causal)
    new_max = jnp.maximum(run_max, jnp.max(scores, axis=-1))
    alpha = jnp.exp(run_max - new_max)
    weights = jnp.exp(scores - new_max[..., None])
    new_sum = run_sum * alpha + jnp.sum(weights, axis=-1)
    new_acc = run_acc * alpha[..., None] + jnp.einsum("bgrqk,bkgd->bgrqd", weights.astype(jnp.bfloat16), value_blk, preferred_element_type=jnp.float32)
    return new_max, new_sum, new_acc


def backward_step(query5, grad5, row_lse, delta, key_blk, value_blk, scale, causal):
    scores = block_scores(query5, key_blk, scale, causal)
    prob_mat = jnp.exp(scores - row_lse[..., None])
    grad_prob = jnp.einsum("bqgrd,bkgd->bgrqk", grad5, value_blk, preferred_element_type=jnp.float32)
    grad_score = (prob_mat * (grad_prob - delta[..., None])).astype(jnp.bfloat16)
    prob_low = prob_mat.astype(jnp.bfloat16)
    dq_part = jnp.einsum("bgrqk,bkgd->bqgrd", grad_score, key_blk, preferred_element_type=jnp.float32) * scale
    dk_part = jnp.einsum("bgrqk,bqgrd->bkgd", grad_score, query5, preferred_element_type=jnp.float32) * scale
    dv_part = jnp.einsum("bgrqk,bqgrd->bkgd", prob_low, grad5, preferred_element_type=jnp.float32)
    return dq_part, dk_part, dv_part


def solution(mesh):
    cp_size = mesh.shape["cp"]
    shift_pairs = [(source, (source + 1) % cp_size) for source in range(cp_size)]

    def attention_shard(queries, keys, values, out_grad):
        batch, tokens, heads, head_dim = queries.shape
        kv_heads = keys.shape[2]
        ratio = heads // kv_heads
        scale = head_dim ** -0.5
        cp_rank = lax.axis_index("cp")
        query5 = queries.reshape(batch, tokens, kv_heads, ratio, head_dim)
        grad5 = out_grad.reshape(batch, tokens, kv_heads, ratio, head_dim)
        stat_shape = (batch, kv_heads, ratio, tokens)
        init_state = (jnp.full(stat_shape, -jnp.inf, jnp.float32), jnp.zeros(stat_shape, jnp.float32), jnp.zeros(stat_shape + (head_dim,), jnp.float32))
        diag_state = forward_step(query5, keys, values, init_state, scale, True)

        def forward_body(step, carry):
            key_cur, value_cur, state = carry
            key_cur = lax.ppermute(key_cur, "cp", shift_pairs)
            value_cur = lax.ppermute(value_cur, "cp", shift_pairs)
            state = lax.cond(step <= cp_rank, lambda prev: forward_step(query5, key_cur, value_cur, prev, scale, False), lambda prev: prev, state)
            return key_cur, value_cur, state

        run_max, run_sum, run_acc = lax.fori_loop(1, cp_size, forward_body, (keys, values, diag_state))[2]
        out5 = (run_acc / run_sum[..., None]).astype(jnp.bfloat16)
        attn_out = jnp.transpose(out5, (0, 3, 1, 2, 4)).reshape(batch, tokens, heads, head_dim)
        row_lse = run_max + jnp.log(run_sum)
        delta = jnp.einsum("bqgrd,bgrqd->bgrq", grad5, out5, preferred_element_type=jnp.float32)

        dq_diag, dk_diag, dv_diag = backward_step(query5, grad5, row_lse, delta, keys, values, scale, True)

        def backward_body(step, carry):
            key_cur, value_cur, dk_cur, dv_cur, dq_acc = carry
            key_cur = lax.ppermute(key_cur, "cp", shift_pairs)
            value_cur = lax.ppermute(value_cur, "cp", shift_pairs)
            dk_cur = lax.ppermute(dk_cur, "cp", shift_pairs)
            dv_cur = lax.ppermute(dv_cur, "cp", shift_pairs)

            def visit(acc_in):
                dk_in, dv_in, dq_in = acc_in
                dq_part, dk_part, dv_part = backward_step(query5, grad5, row_lse, delta, key_cur, value_cur, scale, False)
                return dk_in + dk_part, dv_in + dv_part, dq_in + dq_part

            dk_cur, dv_cur, dq_acc = lax.cond(step <= cp_rank, visit, lambda acc_in: acc_in, (dk_cur, dv_cur, dq_acc))
            return key_cur, value_cur, dk_cur, dv_cur, dq_acc

        carry_out = lax.fori_loop(1, cp_size, backward_body, (keys, values, dk_diag, dv_diag, dq_diag))
        dk_home = lax.ppermute(carry_out[2], "cp", shift_pairs)
        dv_home = lax.ppermute(carry_out[3], "cp", shift_pairs)
        grad_query = carry_out[4].reshape(batch, tokens, heads, head_dim).astype(jnp.bfloat16)
        return attn_out, row_lse.reshape(batch, heads, tokens), grad_query, dk_home.astype(jnp.bfloat16), dv_home.astype(jnp.bfloat16)

    seq_spec = P("dp", "cp")
    return jax.shard_map(attention_shard, mesh=mesh, in_specs=(seq_spec, seq_spec, seq_spec, seq_spec), out_specs=(seq_spec, P("dp", None, "cp"), seq_spec, seq_spec, seq_spec), check_vma=False)
```

profile of v0, /device:TPU:0, one launch (start us, length us, event | category | flops | bytes accessed | tf_op | source)
XLA Modules:
  0.0 4904.4 jit_solution(1566883644953478093)
XLA Ops:
  117.4 1249.9 %while.42 = (s32[]{:T(128)}, bf16[3,384,16,128]{3,1,2,0:T(8,128)(2,1)}, bf16[3,384,16,128]{3,1,2,0:T(8,128)(2,1)}, f32[3,16,2,384]{3,2,1,0:T(2,128)S(1)}, f32[3,...) while((s32[]{:T(128)}, ...), condition=%wide.region_7.8_spmd, body=%wide.region_2.7_spmd.sunk | while | flops 7370514432 | bytes 285475072 | solution.py:63
  120.9 52.1 %collective-permute-done = bf16[3,384,16,128]{3,1,2,0:T(8,128)(2,1)} collective-permute-done((bf16[3,384,16,128]{3,1,2,0:T(8,128)(2,1)}, bf16[3,384,16,128]{3,1,2,0:T(8,128)(2,1)}, u32[]{:S(2)}, u32[]{:S(2)}) %collective-permute-start) | collective-permute-done | bytes 4718624 | tf_op jit(solution)/shard_map/while/body/eval_jaxpr/ppermute | solution.py:58
  173.0 50.6 %collective-permute-done.1 = bf16[3,384,16,128]{3,1,2,0:T(8,128)(2,1)} collective-permute-done((bf16[3,384,16,128]{3,1,2,0:T(8,128)(2,1)}, bf16[3,384,16,128]{3,1,2,0:T(8,128)(2,1)}, u32[]{:S(2)}, u32[]{:S(2)}) %collective-permute-start.1) | collective-permute-done | bytes 4718624 | tf_op jit(solution)/shard_map/while/body/eval_jaxpr/ppermute | solution.py:59
  233.6 76.2 %collective-permute-start = (bf16[3,384,16,128]{3,1,2,0:T(8,128)(2,1)}, bf16[3,384,16,128]{3,1,2,0:T(8,128)(2,1)}, u32[]{:S(2)}, u32[]{:S(2)}) collective-permute-start(bf16[3,384,16,128]{3,1,2,0:T(8,128)(2,1)} %get-tuple-element.632), channel_id=1, source_target_pairs={{0,1},{1,2},{2,3},{3,4},{4,5},{5,6},{6,7},{7,0}} | collective-permute-start | bytes 14155784 | tf_op jit(solution)/shard_map/while/body/eval_jaxpr/ppermute | solution.py:58
  361.9 50.6 %collective-permute-done.1 = bf16[3,384,16,128]{3,1,2,0:T(8,128)(2,1)} collective-permute-done((bf16[3,384,16,128]{3,1,2,0:T(8,128)(2,1)}, bf16[3,384,16,128]{3,1,2,0:T(8,128)(2,1)}, u32[]{:S(2)}, u32[]{:S(2)}) %collective-permute-start.1) | collective-permute-done | bytes 4718624 | tf_op jit(solution)/shard_map/while/body/eval_jaxpr/ppermute | solution.py:59
  424.0 79.8 %collective-permute-start.1 = (bf16[3,384,16,128]{3,1,2,0:T(8,128)(2,1)}, bf16[3,384,16,128]{3,1,2,0:T(8,128)(2,1)}, u32[]{:S(2)}, u32[]{:S(2)}) collective-permute-start(bf16[3,384,16,128]{3,1,2,0:T(8,128)(2,1)} %get-tuple-element.633), channel_id=1, source_target_pairs={{0,1},{1,2},{2,3},{3,4},{4,5},{5,6},{6,7},{7,0}} | collective-permute-start | bytes 14155784 | tf_op jit(solution)/shard_map/while/body/eval_jaxpr/ppermute | solution.py:59
  550.9 50.6 %collective-permute-done.1 = bf16[3,384,16,128]{3,1,2,0:T(8,128)(2,1)} collective-permute-done((bf16[3,384,16,128]{3,1,2,0:T(8,128)(2,1)}, bf16[3,384,16,128]{3,1,2,0:T(8,128)(2,1)}, u32[]{:S(2)}, u32[]{:S(2)}) %collective-permute-start.1) | collective-permute-done | bytes 4718624 | tf_op jit(solution)/shard_map/while/body/eval_jaxpr/ppermute | solution.py:59
  618.0 121.9 %collective-permute-done = bf16[3,384,16,128]{3,1,2,0:T(8,128)(2,1)} collective-permute-done((bf16[3,384,16,128]{3,1,2,0:T(8,128)(2,1)}, bf16[3,384,16,128]{3,1,2,0:T(8,128)(2,1)}, u32[]{:S(2)}, u32[]{:S(2)}) %collective-permute-start) | collective-permute-done | bytes 4718624 | tf_op jit(solution)/shard_map/while/body/eval_jaxpr/ppermute | solution.py:58
  739.8 50.6 %collective-permute-done.1 = bf16[3,384,16,128]{3,1,2,0:T(8,128)(2,1)} collective-permute-done((bf16[3,384,16,128]{3,1,2,0:T(8,128)(2,1)}, bf16[3,384,16,128]{3,1,2,0:T(8,128)(2,1)}, u32[]{:S(2)}, u32[]{:S(2)}) %collective-permute-start.1) | collective-permute-done | bytes 4718624 | tf_op jit(solution)/shard_map/while/body/eval_jaxpr/ppermute | solution.py:59
  800.5 128.3 %collective-permute-done = bf16[3,384,16,128]{3,1,2,0:T(8,128)(2,1)} collective-permute-done((bf16[3,384,16,128]{3,1,2,0:T(8,128)(2,1)}, bf16[3,384,16,128]{3,1,2,0:T(8,128)(2,1)}, u32[]{:S(2)}, u32[]{:S(2)}) %collective-permute-start) | collective-permute-done | bytes 4718624 | tf_op jit(solution)/shard_map/while/body/eval_jaxpr/ppermute | solution.py:58
  989.4 128.3 %collective-permute-done = bf16[3,384,16,128]{3,1,2,0:T(8,128)(2,1)} collective-permute-done((bf16[3,384,16,128]{3,1,2,0:T(8,128)(2,1)}, bf16[3,384,16,128]{3,1,2,0:T(8,128)(2,1)}, u32[]{:S(2)}, u32[]{:S(2)}) %collective-permute-start) | collective-permute-done | bytes 4718624 | tf_op jit(solution)/shard_map/while/body/eval_jaxpr/ppermute | solution.py:58
  1117.7 50.6 %collective-permute-done.1 = bf16[3,384,16,128]{3,1,2,0:T(8,128)(2,1)} collective-permute-done((bf16[3,384,16,128]{3,1,2,0:T(8,128)(2,1)}, bf16[3,384,16,128]{3,1,2,0:T(8,128)(2,1)}, u32[]{:S(2)}, u32[]{:S(2)}) %collective-permute-start.1) | collective-permute-done | bytes 4718624 | tf_op jit(solution)/shard_map/while/body/eval_jaxpr/ppermute | solution.py:59
  1178.3 128.3 %collective-permute-done = bf16[3,384,16,128]{3,1,2,0:T(8,128)(2,1)} collective-permute-done((bf16[3,384,16,128]{3,1,2,0:T(8,128)(2,1)}, bf16[3,384,16,128]{3,1,2,0:T(8,128)(2,1)}, u32[]{:S(2)}, u32[]{:S(2)}) %collective-permute-start) | collective-permute-done | bytes 4718624 | tf_op jit(solution)/shard_map/while/body/eval_jaxpr/ppermute | solution.py:58
  1306.7 50.6 %collective-permute-done.1 = bf16[3,384,16,128]{3,1,2,0:T(8,128)(2,1)} collective-permute-done((bf16[3,384,16,128]{3,1,2,0:T(8,128)(2,1)}, bf16[3,384,16,128]{3,1,2,0:T(8,128)(2,1)}, u32[]{:S(2)}, u32[]{:S(2)}) %collective-permute-start.1) | collective-permute-done | bytes 4718624 | tf_op jit(solution)/shard_map/while/body/eval_jaxpr/ppermute | solution.py:59
  1492.0 3155.1 %while.43 = (s32[]{:T(128)}, bf16[3,384,16,128]{3,1,2,0:T(8,128)(2,1)}, bf16[3,384,16,128]{3,1,2,0:T(8,128)(2,1)}, f32[3,384,16,128]{3,1,2,0:T(8,128)}, f32[3,38...) while((s32[]{:T(128)}, ...), condition=%wide.region_11.12_spmd, body=%wide.region_8.11_spmd.sunk | while | flops 18249154560 | bytes 552518016 | solution.py:86
  1492.4 330.4 %collective-permute-done.2 = bf16[3,384,16,128]{3,1,2,0:T(8,128)(2,1)} collective-permute-done((bf16[3,384,16,128]{3,1,2,0:T(8,128)(2,1)}, bf16[3,384,16,128]{3,1,2,0:T(8,128)(2,1)}, u32[]{:S(2)}, u32[]{:S(2)}) %collective-permute-start.2) | collective-permute-done | bytes 4718624 | tf_op jit(solution)/shard_map/while/body/eval_jaxpr/ppermute | solution.py:73
  1895.1 386.3 %collective-permute-done.2 = bf16[3,384,16,128]{3,1,2,0:T(8,128)(2,1)} collective-permute-done((bf16[3,384,16,128]{3,1,2,0:T(8,128)(2,1)}, bf16[3,384,16,128]{3,1,2,0:T(8,128)(2,1)}, u32[]{:S(2)}, u32[]{:S(2)}) %collective-permute-start.2) | collective-permute-done | bytes 4718624 | tf_op jit(solution)/shard_map/while/body/eval_jaxpr/ppermute | solution.py:73
  2353.8 386.3 %collective-permute-done.2 = bf16[3,384,16,128]{3,1,2,0:T(8,128)(2,1)} collective-permute-done((bf16[3,384,16,128]{3,1,2,0:T(8,128)(2,1)}, bf16[3,384,16,128]{3,1,2,0:T(8,128)(2,1)}, u32[]{:S(2)}, u32[]{:S(2)}) %collective-permute-start.2) | collective-permute-done | bytes 4718624 | tf_op jit(solution)/shard_map/while/body/eval_jaxpr/ppermute | solution.py:73
  2812.4 386.3 %collective-permute-done.2 = bf16[3,384,16,128]{3,1,2,0:T(8,128)(2,1)} collective-permute-done((bf16[3,384,16,128]{3,1,2,0:T(8,128)(2,1)}, bf16[3,384,16,128]{3,1,2,0:T(8,128)(2,1)}, u32[]{:S(2)}, u32[]{:S(2)}) %collective-permute-start.2) | collective-permute-done | bytes 4718624 | tf_op jit(solution)/shard_map/while/body/eval_jaxpr/ppermute | solution.py:73
  3271.1 386.3 %collective-permute-done.2 = bf16[3,384,16,128]{3,1,2,0:T(8,128)(2,1)} collective-permute-done((bf16[3,384,16,128]{3,1,2,0:T(8,128)(2,1)}, bf16[3,384,16,128]{3,1,2,0:T(8,128)(2,1)}, u32[]{:S(2)}, u32[]{:S(2)}) %collective-permute-start.2) | collective-permute-done | bytes 4718624 | tf_op jit(solution)/shard_map/while/body/eval_jaxpr/ppermute | solution.py:73
  3729.7 386.3 %collective-permute-done.2 = bf16[3,384,16,128]{3,1,2,0:T(8,128)(2,1)} collective-permute-done((bf16[3,384,16,128]{3,1,2,0:T(8,128)(2,1)}, bf16[3,384,16,128]{3,1,2,0:T(8,128)(2,1)}, u32[]{:S(2)}, u32[]{:S(2)}) %collective-permute-start.2) | collective-permute-done | bytes 4718624 | tf_op jit(solution)/shard_map/while/body/eval_jaxpr/ppermute | solution.py:73
  4188.4 386.3 %collective-permute-done.2 = bf16[3,384,16,128]{3,1,2,0:T(8,128)(2,1)} collective-permute-done((bf16[3,384,16,128]{3,1,2,0:T(8,128)(2,1)}, bf16[3,384,16,128]{3,1,2,0:T(8,128)(2,1)}, u32[]{:S(2)}, u32[]{:S(2)}) %collective-permute-start.2) | collective-permute-done | bytes 4718624 | tf_op jit(solution)/shard_map/while/body/eval_jaxpr/ppermute | solution.py:73
  4731.4 111.3 %collective-permute-done.6 = bf16[3,384,16,128]{3,2,1,0:T(8,128)(2,1)} collective-permute-done((bf16[3,384,16,128]{3,2,1,0:T(8,128)(2,1)}, bf16[3,384,16,128]{3,2,1,0:T(8,128)(2,1)}, u32[]{:S(2)}, u32[]{:S(2)}) %collective-permute-start.6) | collective-permute-done | bytes 4718624 | tf_op jit(solution)/shard_map/ppermute | solution.py:87
  4842.7 50.6 %collective-permute-done.7 = bf16[3,384,16,128]{3,2,1,0:T(8,128)(2,1)} collective-permute-done((bf16[3,384,16,128]{3,2,1,0:T(8,128)(2,1)}, bf16[3,384,16,128]{3,2,1,0:T(8,128)(2,1)}, u32[]{:S(2)}, u32[]{:S(2)}) %collective-permute-start.7) | collective-permute-done | bytes 4718624 | tf_op jit(solution)/shard_map/ppermute | solution.py:88
  (162 shorter events, 1074.4 us)
Async XLA Ops:
  1895.1 441.9 %collective-permute-start.4 = (f32[3,384,16,128]{3,1,2,0:T(8,128)}, f32[3,384,16,128]{3,1,2,0:T(8,128)}, u32[]{:S(2)}, u32[]{:S(2)}) collective-permute-start(f32[3,384,16,128]{3,1,2,0:T(8,128)} %get-tuple-element.664), channel_id=1, source_target_pairs={{0,1},{1,2},{2,3},{3,4},{4,5},{5,6},{6,7},{7,0}} | collective-permute-start | bytes 28311560 | tf_op jit(solution)/shard_map/while/body/eval_jaxpr/ppermute | solution.py:75
  1895.1 441.9 %collective-permute-start.5 = (f32[3,384,16,128]{3,1,2,0:T(8,128)}, f32[3,384,16,128]{3,1,2,0:T(8,128)}, u32[]{:S(2)}, u32[]{:S(2)}) collective-permute-start(f32[3,384,16,128]{3,1,2,0:T(8,128)} %get-tuple-element.665), channel_id=1, source_target_pairs={{0,1},{1,2},{2,3},{3,4},{4,5},{5,6},{6,7},{7,0}} | collective-permute-start | bytes 28311560 | tf_op jit(solution)/shard_map/while/body/eval_jaxpr/ppermute | solution.py:76
  1895.1 386.3 %collective-permute-start.2 = (bf16[3,384,16,128]{3,1,2,0:T(8,128)(2,1)}, bf16[3,384,16,128]{3,1,2,0:T(8,128)(2,1)}, u32[]{:S(2)}, u32[]{:S(2)}) collective-permute-start(bf16[3,384,16,128]{3,1,2,0:T(8,128)(2,1)} %get-tuple-element.662), channel_id=1, source_target_pairs={{0,1},{1,2},{2,3},{3,4},{4,5},{5,6},{6,7},{7,0}} | collective-permute-start | bytes 14155784 | tf_op jit(solution)/shard_map/while/body/eval_jaxpr/ppermute | solution.py:73
  1895.1 436.9 %collective-permute-start.3 = (bf16[3,384,16,128]{3,1,2,0:T(8,128)(2,1)}, bf16[3,384,16,128]{3,1,2,0:T(8,128)(2,1)}, u32[]{:S(2)}, u32[]{:S(2)}) collective-permute-start(bf16[3,384,16,128]{3,1,2,0:T(8,128)(2,1)} %get-tuple-element.663), channel_id=1, source_target_pairs={{0,1},{1,2},{2,3},{3,4},{4,5},{5,6},{6,7},{7,0}} | collective-permute-start | bytes 14155784 | tf_op jit(solution)/shard_map/while/body/eval_jaxpr/ppermute | solution.py:74
  2353.7 441.9 %collective-permute-start.4 = (f32[3,384,16,128]{3,1,2,0:T(8,128)}, f32[3,384,16,128]{3,1,2,0:T(8,128)}, u32[]{:S(2)}, u32[]{:S(2)}) collective-permute-start(f32[3,384,16,128]{3,1,2,0:T(8,128)} %get-tuple-element.664), channel_id=1, source_target_pairs={{0,1},{1,2},{2,3},{3,4},{4,5},{5,6},{6,7},{7,0}} | collective-permute-start | bytes 28311560 | tf_op jit(solution)/shard_map/while/body/eval_jaxpr/ppermute | solution.py:75
  2353.7 441.9 %collective-permute-start.5 = (f32[3,384,16,128]{3,1,2,0:T(8,128)}, f32[3,384,16,128]{3,1,2,0:T(8,128)}, u32[]{:S(2)}, u32[]{:S(2)}) collective-permute-start(f32[3,384,16,128]{3,1,2,0:T(8,128)} %get-tuple-element.665), channel_id=1, source_target_pairs={{0,1},{1,2},{2,3},{3,4},{4,5},{5,6},{6,7},{7,0}} | collective-permute-start | bytes 28311560 | tf_op jit(solution)/shard_map/while/body/eval_jaxpr/ppermute | solution.py:76
  2353.7 386.4 %collective-permute-start.2 = (bf16[3,384,16,128]{3,1,2,0:T(8,128)(2,1)}, bf16[3,384,16,128]{3,1,2,0:T(8,128)(2,1)}, u32[]{:S(2)}, u32[]{:S(2)}) collective-permute-start(bf16[3,384,16,128]{3,1,2,0:T(8,128)(2,1)} %get-tuple-element.662), channel_id=1, source_target_pairs={{0,1},{1,2},{2,3},{3,4},{4,5},{5,6},{6,7},{7,0}} | collective-permute-start | bytes 14155784 | tf_op jit(solution)/shard_map/while/body/eval_jaxpr/ppermute | solution.py:73
  2353.7 436.9 %collective-permute-start.3 = (bf16[3,384,16,128]{3,1,2,0:T(8,128)(2,1)}, bf16[3,384,16,128]{3,1,2,0:T(8,128)(2,1)}, u32[]{:S(2)}, u32[]{:S(2)}) collective-permute-start(bf16[3,384,16,128]{3,1,2,0:T(8,128)(2,1)} %get-tuple-element.663), channel_id=1, source_target_pairs={{0,1},{1,2},{2,3},{3,4},{4,5},{5,6},{6,7},{7,0}} | collective-permute-start | bytes 14155784 | tf_op jit(solution)/shard_map/while/body/eval_jaxpr/ppermute | solution.py:74
  2812.3 441.9 %collective-permute-start.4 = (f32[3,384,16,128]{3,1,2,0:T(8,128)}, f32[3,384,16,128]{3,1,2,0:T(8,128)}, u32[]{:S(2)}, u32[]{:S(2)}) collective-permute-start(f32[3,384,16,128]{3,1,2,0:T(8,128)} %get-tuple-element.664), channel_id=1, source_target_pairs={{0,1},{1,2},{2,3},{3,4},{4,5},{5,6},{6,7},{7,0}} | collective-permute-start | bytes 28311560 | tf_op jit(solution)/shard_map/while/body/eval_jaxpr/ppermute | solution.py:75
  2812.4 441.9 %collective-permute-start.5 = (f32[3,384,16,128]{3,1,2,0:T(8,128)}, f32[3,384,16,128]{3,1,2,0:T(8,128)}, u32[]{:S(2)}, u32[]{:S(2)}) collective-permute-start(f32[3,384,16,128]{3,1,2,0:T(8,128)} %get-tuple-element.665), channel_id=1, source_target_pairs={{0,1},{1,2},{2,3},{3,4},{4,5},{5,6},{6,7},{7,0}} | collective-permute-start | bytes 28311560 | tf_op jit(solution)/shard_map/while/body/eval_jaxpr/ppermute | solution.py:76
  2812.4 386.3 %collective-permute-start.2 = (bf16[3,384,16,128]{3,1,2,0:T(8,128)(2,1)}, bf16[3,384,16,128]{3,1,2,0:T(8,128)(2,1)}, u32[]{:S(2)}, u32[]{:S(2)}) collective-permute-start(bf16[3,384,16,128]{3,1,2,0:T(8,128)(2,1)} %get-tuple-element.662), channel_id=1, source_target_pairs={{0,1},{1,2},{2,3},{3,4},{4,5},{5,6},{6,7},{7,0}} | collective-permute-start | bytes 14155784 | tf_op jit(solution)/shard_map/while/body/eval_jaxpr/ppermute | solution.py:73
  2812.4 436.9 %collective-permute-start.3 = (bf16[3,384,16,128]{3,1,2,0:T(8,128)(2,1)}, bf16[3,384,16,128]{3,1,2,0:T(8,128)(2,1)}, u32[]{:S(2)}, u32[]{:S(2)}) collective-permute-start(bf16[3,384,16,128]{3,1,2,0:T(8,128)(2,1)} %get-tuple-element.663), channel_id=1, source_target_pairs={{0,1},{1,2},{2,3},{3,4},{4,5},{5,6},{6,7},{7,0}} | collective-permute-start | bytes 14155784 | tf_op jit(solution)/shard_map/while/body/eval_jaxpr/ppermute | solution.py:74
  3271.0 441.9 %collective-permute-start.4 = (f32[3,384,16,128]{3,1,2,0:T(8,128)}, f32[3,384,16,128]{3,1,2,0:T(8,128)}, u32[]{:S(2)}, u32[]{:S(2)}) collective-permute-start(f32[3,384,16,128]{3,1,2,0:T(8,128)} %get-tuple-element.664), channel_id=1, source_target_pairs={{0,1},{1,2},{2,3},{3,4},{4,5},{5,6},{6,7},{7,0}} | collective-permute-start | bytes 28311560 | tf_op jit(solution)/shard_map/while/body/eval_jaxpr/ppermute | solution.py:75
  3271.0 441.9 %collective-permute-start.5 = (f32[3,384,16,128]{3,1,2,0:T(8,128)}, f32[3,384,16,128]{3,1,2,0:T(8,128)}, u32[]{:S(2)}, u32[]{:S(2)}) collective-permute-start(f32[3,384,16,128]{3,1,2,0:T(8,128)} %get-tuple-element.665), channel_id=1, source_target_pairs={{0,1},{1,2},{2,3},{3,4},{4,5},{5,6},{6,7},{7,0}} | collective-permute-start | bytes 28311560 | tf_op jit(solution)/shard_map/while/body/eval_jaxpr/ppermute | solution.py:76
  3271.0 386.4 %collective-permute-start.2 = (bf16[3,384,16,128]{3,1,2,0:T(8,128)(2,1)}, bf16[3,384,16,128]{3,1,2,0:T(8,128)(2,1)}, u32[]{:S(2)}, u32[]{:S(2)}) collective-permute-start(bf16[3,384,16,128]{3,1,2,0:T(8,128)(2,1)} %get-tuple-element.662), channel_id=1, source_target_pairs={{0,1},{1,2},{2,3},{3,4},{4,5},{5,6},{6,7},{7,0}} | collective-permute-start | bytes 14155784 | tf_op jit(solution)/shard_map/while/body/eval_jaxpr/ppermute | solution.py:73
  3271.0 436.9 %collective-permute-start.3 = (bf16[3,384,16,128]{3,1,2,0:T(8,128)(2,1)}, bf16[3,384,16,128]{3,1,2,0:T(8,128)(2,1)}, u32[]{:S(2)}, u32[]{:S(2)}) collective-permute-start(bf16[3,384,16,128]{3,1,2,0:T(8,128)(2,1)} %get-tuple-element.663), channel_id=1, source_target_pairs={{0,1},{1,2},{2,3},{3,4},{4,5},{5,6},{6,7},{7,0}} | collective-permute-start | bytes 14155784 | tf_op jit(solution)/shard_map/while/body/eval_jaxpr/ppermute | solution.py:74
  3729.6 441.9 %collective-permute-start.4 = (f32[3,384,16,128]{3,1,2,0:T(8,128)}, f32[3,384,16,128]{3,1,2,0:T(8,128)}, u32[]{:S(2)}, u32[]{:S(2)}) collective-permute-start(f32[3,384,16,128]{3,1,2,0:T(8,128)} %get-tuple-element.664), channel_id=1, source_target_pairs={{0,1},{1,2},{2,3},{3,4},{4,5},{5,6},{6,7},{7,0}} | collective-permute-start | bytes 28311560 | tf_op jit(solution)/shard_map/while/body/eval_jaxpr/ppermute | solution.py:75
  3729.7 441.9 %collective-permute-start.5 = (f32[3,384,16,128]{3,1,2,0:T(8,128)}, f32[3,384,16,128]{3,1,2,0:T(8,128)}, u32[]{:S(2)}, u32[]{:S(2)}) collective-permute-start(f32[3,384,16,128]{3,1,2,0:T(8,128)} %get-tuple-element.665), channel_id=1, source_target_pairs={{0,1},{1,2},{2,3},{3,4},{4,5},{5,6},{6,7},{7,0}} | collective-permute-start | bytes 28311560 | tf_op jit(solution)/shard_map/while/body/eval_jaxpr/ppermute | solution.py:76
  3729.7 386.3 %collective-permute-start.2 = (bf16[3,384,16,128]{3,1,2,0:T(8,128)(2,1)}, bf16[3,384,16,128]{3,1,2,0:T(8,128)(2,1)}, u32[]{:S(2)}, u32[]{:S(2)}) collective-permute-start(bf16[3,384,16,128]{3,1,2,0:T(8,128)(2,1)} %get-tuple-element.662), channel_id=1, source_target_pairs={{0,1},{1,2},{2,3},{3,4},{4,5},{5,6},{6,7},{7,0}} | collective-permute-start | bytes 14155784 | tf_op jit(solution)/shard_map/while/body/eval_jaxpr/ppermute | solution.py:73
  3729.7 436.9 %collective-permute-start.3 = (bf16[3,384,16,128]{3,1,2,0:T(8,128)(2,1)}, bf16[3,384,16,128]{3,1,2,0:T(8,128)(2,1)}, u32[]{:S(2)}, u32[]{:S(2)}) collective-permute-start(bf16[3,384,16,128]{3,1,2,0:T(8,128)(2,1)} %get-tuple-element.663), channel_id=1, source_target_pairs={{0,1},{1,2},{2,3},{3,4},{4,5},{5,6},{6,7},{7,0}} | collective-permute-start | bytes 14155784 | tf_op jit(solution)/shard_map/while/body/eval_jaxpr/ppermute | solution.py:74
  4188.3 441.9 %collective-permute-start.4 = (f32[3,384,16,128]{3,1,2,0:T(8,128)}, f32[3,384,16,128]{3,1,2,0:T(8,128)}, u32[]{:S(2)}, u32[]{:S(2)}) collective-permute-start(f32[3,384,16,128]{3,1,2,0:T(8,128)} %get-tuple-element.664), channel_id=1, source_target_pairs={{0,1},{1,2},{2,3},{3,4},{4,5},{5,6},{6,7},{7,0}} | collective-permute-start | bytes 28311560 | tf_op jit(solution)/shard_map/while/body/eval_jaxpr/ppermute | solution.py:75
  4188.3 441.9 %collective-permute-start.5 = (f32[3,384,16,128]{3,1,2,0:T(8,128)}, f32[3,384,16,128]{3,1,2,0:T(8,128)}, u32[]{:S(2)}, u32[]{:S(2)}) collective-permute-start(f32[3,384,16,128]{3,1,2,0:T(8,128)} %get-tuple-element.665), channel_id=1, source_target_pairs={{0,1},{1,2},{2,3},{3,4},{4,5},{5,6},{6,7},{7,0}} | collective-permute-start | bytes 28311560 | tf_op jit(solution)/shard_map/while/body/eval_jaxpr/ppermute | solution.py:76
  4188.3 386.4 %collective-permute-start.2 = (bf16[3,384,16,128]{3,1,2,0:T(8,128)(2,1)}, bf16[3,384,16,128]{3,1,2,0:T(8,128)(2,1)}, u32[]{:S(2)}, u32[]{:S(2)}) collective-permute-start(bf16[3,384,16,128]{3,1,2,0:T(8,128)(2,1)} %get-tuple-element.662), channel_id=1, source_target_pairs={{0,1},{1,2},{2,3},{3,4},{4,5},{5,6},{6,7},{7,0}} | collective-permute-start | bytes 14155784 | tf_op jit(solution)/shard_map/while/body/eval_jaxpr/ppermute | solution.py:73
  4188.3 436.9 %collective-permute-start.3 = (bf16[3,384,16,128]{3,1,2,0:T(8,128)(2,1)}, bf16[3,384,16,128]{3,1,2,0:T(8,128)(2,1)}, u32[]{:S(2)}, u32[]{:S(2)}) collective-permute-start(bf16[3,384,16,128]{3,1,2,0:T(8,128)(2,1)} %get-tuple-element.663), channel_id=1, source_target_pairs={{0,1},{1,2},{2,3},{3,4},{4,5},{5,6},{6,7},{7,0}} | collective-permute-start | bytes 14155784 | tf_op jit(solution)/shard_map/while/body/eval_jaxpr/ppermute | solution.py:74
  (27 other events, 5267.3 us)
where the time goes:
time: 4910 us; the launch traced here: 4900 us
  waiting for transfers between devices  4140 us (84%)
  local copies, waits for them, and re-layouts  385 us (8%)
  starting transfers between devices  170 us (3%)
  matrix products  164 us (3%)
    ppermute x7, waiting for transfers between devices, backward_body(): key_cur = lax.ppermute(key_cur, 'cp', shift_pairs)  2650 us
    ppermute x7, waiting for transfers between devices, forward_body(): key_cur = lax.ppermute(key_cur, 'cp', shift_pairs)  656 us
    ppermute x7, waiting for transfers between devices, forward_body(): value_cur = lax.ppermute(value_cur, 'cp', shift_pairs)  354 us
    ppermute x7, waiting for transfers between devices, backward_body(): value_cur = lax.ppermute(value_cur, 'cp', shift_pairs)  319 us
    while x42, local copies, waits for them, and re-layouts  258 us
    ppermute x1, waiting for transfers between devices, attention_shard(): dk_home = lax.ppermute(carry_out[2], 'cp', shift_pairs)  111 us
  transfers between devices with their start and end apart: 44, of which 30 were waited for; matrix products, arithmetic and copies ran while one was open for 3% of the time, Pallas kernels for 0%

commit v1 on v0

v1 whole, which is shorter than its diff:
```python
import jax
import jax.numpy as jnp
from jax import lax
from jax.experimental import pallas as pl
from jax.experimental.pallas import tpu as pltpu
from jax.sharding import PartitionSpec as P


LOG2E = 1.4426950408889634
BQ = 256
BK = 512
TB = 64


def dot_nt(lhs, rhs):
    return lax.dot_general(lhs, rhs, (((1,), (1,)), ((), ())), preferred_element_type=jnp.float32)


def dot_nn(lhs, rhs):
    return lax.dot_general(lhs, rhs, (((1,), (0,)), ((), ())), preferred_element_type=jnp.float32)


def attention_kernel(x_ref, y_ref, lse_ref, q_cat, g_cat, k_t, v_t, s_buf, ot_acc, dqt_acc, dk_acc, dv_acc):
    seq = x_ref.shape[0]
    dim = k_t.shape[0]
    width = 2 * BQ
    scale = dim ** -0.5
    scale2 = scale * LOG2E
    q_col, g_col, k_col, v_col = 0, 2 * dim, 4 * dim, 5 * dim

    def prepare(blk, carry):
        rows = pl.ds(pl.multiple_of(blk * BK, BK), BK)
        k_t[:, rows] = x_ref[rows, k_col:k_col + dim].T
        v_t[:, rows] = x_ref[rows, v_col:v_col + dim].T
        dk_acc[rows, :] = jnp.zeros((BK, dim), jnp.float32)
        dv_acc[rows, :] = jnp.zeros((BK, dim), jnp.float32)
        return carry

    lax.fori_loop(0, seq // BK, prepare, 0)

    def fold(tile, op):
        return op(tile.reshape(BK // 8, 8, width), axis=0)

    def query_block(blk, carry):
        rows = pl.ds(pl.multiple_of(blk * BQ, BQ), BQ)
        for head in range(2):
            q_cat[head * BQ:(head + 1) * BQ, :] = x_ref[rows, q_col + head * dim:q_col + (head + 1) * dim]
            g_cat[head * BQ:(head + 1) * BQ, :] = x_ref[rows, g_col + head * dim:g_col + (head + 1) * dim]
        last = (blk * BQ) // BK

        def key_rows(step):
            return pl.ds(pl.multiple_of(step * BK, BK), BK)

        def score_step(step, run_max):
            scores = dot_nt(x_ref[key_rows(step), k_col:k_col + dim], q_cat[...])
            s_buf[key_rows(step), :] = scores
            return jnp.maximum(run_max, fold(scores, jnp.max))

        run_max = lax.fori_loop(0, last, score_step, jnp.full((8, width), -jnp.inf, jnp.float32))
        scores = dot_nt(x_ref[key_rows(last), k_col:k_col + dim], q_cat[...])
        key_pos = last * BK + lax.broadcasted_iota(jnp.int32, (BK, width), 0)
        query_pos = blk * BQ + lax.broadcasted_iota(jnp.int32, (BK, width), 1) % BQ
        scores = jnp.where(key_pos <= query_pos, scores, -jnp.inf)
        s_buf[key_rows(last), :] = scores
        run_max = jnp.maximum(run_max, fold(scores, jnp.max))
        row_max = jnp.max(run_max, axis=0, keepdims=True)
        shift = row_max * scale2
        ot_acc[...] = jnp.zeros_like(ot_acc)

        def value_step(step, run_sum):
            weights = jnp.exp2(s_buf[key_rows(step), :] * scale2 - shift)
            ot_acc[...] += dot_nn(v_t[:, key_rows(step)], weights.astype(jnp.bfloat16))
            return run_sum + fold(weights, jnp.sum)

        run_sum = lax.fori_loop(0, last + 1, value_step, jnp.zeros((8, width), jnp.float32))
        row_sum = jnp.sum(run_sum, axis=0, keepdims=True)
        out_t = (ot_acc[...] / row_sum).astype(jnp.bfloat16)
        row_lse = row_max * scale + jnp.log(row_sum)
        lse2 = row_lse * LOG2E
        out_f = out_t.astype(jnp.float32)
        grad_t = g_cat[...].astype(jnp.float32).T
        delta = jnp.sum(out_f * grad_t, axis=0, keepdims=True)
        out_n = out_f.T.astype(jnp.bfloat16)
        for head in range(2):
            y_ref[rows, head * dim:(head + 1) * dim] = out_n[head * BQ:(head + 1) * BQ, :]
            lse_ref[0, head:head + 1, rows] = row_lse[:, head * BQ:(head + 1) * BQ]
        dqt_acc[...] = jnp.zeros_like(dqt_acc)

        def grad_step(step, inner):
            probs = jnp.exp2(s_buf[key_rows(step), :] * scale2 - lse2)
            grad_prob = dot_nt(x_ref[key_rows(step), v_col:v_col + dim], g_cat[...])
            grad_score = (probs * (grad_prob - delta)).astype(jnp.bfloat16)
            dv_acc[key_rows(step), :] += dot_nn(probs.astype(jnp.bfloat16), g_cat[...])
            dk_acc[key_rows(step), :] += dot_nn(grad_score, q_cat[...])
            dqt_acc[...] += dot_nn(k_t[:, key_rows(step)], grad_score)
            return inner

        lax.fori_loop(0, last + 1, grad_step, 0)
        dq_n = (dqt_acc[...] * scale).T.astype(jnp.bfloat16)
        for head in range(2):
            y_ref[rows, (2 + head) * dim:(3 + head) * dim] = dq_n[head * BQ:(head + 1) * BQ, :]
        return carry

    lax.fori_loop(0, seq // BQ, query_block, 0)

    def finish(blk, carry):
        rows = pl.ds(pl.multiple_of(blk * BK, BK), BK)
        y_ref[rows, 4 * dim:5 * dim] = (dk_acc[rows, :] * scale).astype(jnp.bfloat16)
        y_ref[rows, 5 * dim:6 * dim] = dv_acc[rows, :].astype(jnp.bfloat16)
        return carry

    lax.fori_loop(0, seq // BK, finish, 0)


def attention_call(packed, groups, dim):
    seq = packed.shape[0]
    wide = 6 * dim
    pairs = groups * 2 * seq * seq // 2
    return pl.pallas_call(
        attention_kernel,
        grid=(groups,),
        in_specs=[pl.BlockSpec((seq, wide), lambda g: (0, g))],
        out_specs=[pl.BlockSpec((seq, wide), lambda g: (0, g)), pl.BlockSpec((1, 2, seq), lambda g: (g, 0, 0))],
        out_shape=[jax.ShapeDtypeStruct((seq, groups * wide), jnp.bfloat16), jax.ShapeDtypeStruct((groups, 2, seq), jnp.float32)],
        scratch_shapes=[
            pltpu.VMEM((2 * BQ, dim), jnp.bfloat16),
            pltpu.VMEM((2 * BQ, dim), jnp.bfloat16),
            pltpu.VMEM((dim, seq), jnp.bfloat16),
            pltpu.VMEM((dim, seq), jnp.bfloat16),
            pltpu.VMEM((seq, 2 * BQ), jnp.float32),
            pltpu.VMEM((dim, 2 * BQ), jnp.float32),
            pltpu.VMEM((dim, 2 * BQ), jnp.float32),
            pltpu.VMEM((seq, dim), jnp.float32),
            pltpu.VMEM((seq, dim), jnp.float32),
        ],
        compiler_params=pltpu.CompilerParams(dimension_semantics=("arbitrary",), vmem_limit_bytes=60 * 1024 * 1024),
        cost_estimate=pl.CostEstimate(flops=pairs * dim * 2 * 12, bytes_accessed=packed.size * 4, transcendentals=pairs * 2),
    )(packed)


def pack_kernel(q_ref, g_ref, k_ref, v_ref, o_ref):
    parts, _ = o_ref.shape[:2]
    dim = q_ref.shape[-1]
    groups = k_ref.shape[2] // parts
    wide = 6 * dim
    for ref, first, count in ((q_ref, 0, 2), (g_ref, 2, 2), (k_ref, 4, 1), (v_ref, 5, 1)):
        by_head = pltpu.einshape("thd->htd", ref[0])
        for head in range(ref.shape[2]):
            part, local = divmod(head, groups * count)
            group, lane = divmod(local, count)
            start = group * wide + (first + lane) * dim
            o_ref[part, :, start:start + dim] = by_head[head]


def pack_call(queries, out_grad, keys, values, idx, parts):
    _, tokens, heads, dim = queries.shape
    kv_heads = keys.shape[2]
    width = kv_heads // parts * 6 * dim
    big = pl.BlockSpec((1, TB, heads, dim), lambda i: (idx, i, 0, 0))
    small = pl.BlockSpec((1, TB, kv_heads, dim), lambda i: (idx, i, 0, 0))
    return pl.pallas_call(
        pack_kernel,
        grid=(tokens // TB,),
        in_specs=[big, big, small, small],
        out_specs=pl.BlockSpec((parts, TB, width), lambda i: (0, i, 0)),
        out_shape=jax.ShapeDtypeStruct((parts, tokens, width), jnp.bfloat16),
        compiler_params=pltpu.CompilerParams(dimension_semantics=("arbitrary",), vmem_limit_bytes=62 * 1024 * 1024),
        cost_estimate=pl.CostEstimate(flops=parts * tokens * width * 200, bytes_accessed=parts * tokens * width * 4, transcendentals=0),
    )(queries, out_grad, keys, values)


def unpack_kernel(*refs):
    y_ref = refs[0]
    o_ref, dq_ref, dk_ref, dv_ref = refs[-4:]
    parts = y_ref.shape[0]
    dim = o_ref.shape[-1]
    groups = dk_ref.shape[2] // parts
    wide = 6 * dim
    for ref, first, count in ((o_ref, 0, 2), (dq_ref, 2, 2), (dk_ref, 4, 1), (dv_ref, 5, 1)):
        rows = []
        for head in range(ref.shape[2]):
            part, local = divmod(head, groups * count)
            group, lane = divmod(local, count)
            start = group * wide + (first + lane) * dim
            rows.append(y_ref[part, :, start:start + dim])
        ref[0] = pltpu.einshape("htd->thd", jnp.stack(rows))


def unpack_call(y, prev, idx, batch, heads, kv_heads, dim):
    parts, tokens, width = y.shape
    big = pl.BlockSpec((1, TB, heads, dim), lambda i: (idx, i, 0, 0))
    small = pl.BlockSpec((1, TB, kv_heads, dim), lambda i: (idx, i, 0, 0))
    big_shape = jax.ShapeDtypeStruct((batch, tokens, heads, dim), jnp.bfloat16)
    small_shape = jax.ShapeDtypeStruct((batch, tokens, kv_heads, dim), jnp.bfloat16)
    return pl.pallas_call(
        unpack_kernel,
        grid=(tokens // TB,),
        in_specs=[pl.BlockSpec((parts, TB, width), lambda i: (0, i, 0))] + [pl.BlockSpec(memory_space=pl.ANY)] * len(prev),
        out_specs=[big, big, small, small],
        out_shape=[big_shape, big_shape, small_shape, small_shape],
        input_output_aliases={i + 1: i for i in range(len(prev))},
        compiler_params=pltpu.CompilerParams(dimension_semantics=("arbitrary",), vmem_limit_bytes=62 * 1024 * 1024),
        cost_estimate=pl.CostEstimate(flops=y.size * 200, bytes_accessed=y.size * 4, transcendentals=0),
    )(y, *prev)


def solution(mesh):
    cp_size = mesh.shape["cp"]

    def attention_shard(queries, keys, values, out_grad):
        batch, tokens, heads, dim = queries.shape
        kv_heads = keys.shape[2]
        groups = kv_heads // cp_size
        width = groups * 6 * dim
        ready, sums = [], []
        for idx in range(batch):
            packed = pack_call(queries, out_grad, keys, values, idx, cp_size)
            if idx:
                packed, ready[-1] = lax.optimization_barrier((packed, ready[-1]))
            ready.append(lax.all_to_all(packed, "cp", 0, 0, tiled=True))
        done = []
        for idx in range(batch):
            y, lse = attention_call(ready[idx].reshape(cp_size * tokens, width), groups, dim)
            y = y.reshape(cp_size, tokens, width)
            if idx:
                y, done[-1] = lax.optimization_barrier((y, done[-1]))
            done.append(lax.all_to_all(y, "cp", 0, 0, tiled=True))
            sums.append(lse)
        outs = ()
        for idx in range(batch):
            outs = unpack_call(done[idx], outs, idx, batch, heads, kv_heads, dim)
        lse = jnp.stack(sums).reshape(batch, groups * 2, cp_size, tokens)
        lse = lax.all_to_all(jnp.transpose(lse, (2, 0, 1, 3)), "cp", 0, 0, tiled=True)
        lse = jnp.transpose(lse, (1, 0, 2, 3)).reshape(batch, heads, tokens)
        return outs[0], lse, outs[1], outs[2], outs[3]

    seq_spec = P("dp", "cp")
    return jax.shard_map(attention_shard, mesh=mesh, in_specs=(seq_spec, seq_spec, seq_spec, seq_spec), out_specs=(seq_spec, P("dp", None, "cp"), seq_spec, seq_spec, seq_spec), check_vma=False)
```

time: 4910 us -> 747 us (0.15)
  waiting for transfers between devices: 4140 us -> 285 us
  Pallas kernels: 0 us -> 431 us
  local copies, waits for them, and re-layouts: 385 us -> 1.7 us
  matrix products: 164 us -> 0 us
  starting transfers between devices: 170 us -> 26.3 us
    ppermute x44 -> x0, waiting for transfers between devices: 4140 us -> none  [the longest x7 2650 us: backward_body(): key_cur = lax.ppermute(key_cur, 'cp', shift_pairs)]
    pallas_call x0 -> x9, Pallas kernels: none -> 431 us  [the longest x3 377 us: attention_call(): pl.pallas_call(attention_kernel, grid=(groups,), in_specs=[pl.BlockSpec((...]
    while x46 -> x0, local copies, waits for them, and re-layouts: 286 us -> none
    all_to_all x0 -> x7, waiting for transfers between devices: none -> 285 us  [the longest x3 183 us: attention_shard(): done.append(lax.all_to_all(y, 'cp', 0, 0, tiled=True))]
    ppermute x44 -> x0, starting transfers between devices: 170 us -> none  [the longest x7 87.4 us: forward_body(): value_cur = lax.ppermute(value_cur, 'cp', shift_pairs)]
    dot_general x6 -> x0, matrix products: 164 us -> none  [the longest x1 37.7 us: backward_step(): jnp.einsum('bqgrd,bkgd->bgrqk', grad5, value_blk, preferred_element_type=...]
  transfers between devices with their start and end apart: 44 -> 7, of which waited for: 30 -> 4; matrix products, arithmetic and copies ran while one was open for 3% -> 0% of each run, Pallas kernels for 0% -> 55%
where the time goes in v1:
time: 747 us; the launch traced here: 746 us
  Pallas kernels  431 us (58%)
  waiting for transfers between devices  285 us (38%)
  starting transfers between devices  26.3 us (4%)
    pallas_call x3, Pallas kernels, attention_call(): pl.pallas_call(attention_kernel, grid=(groups,), in_specs=[pl.BlockSpec((...  377 us
    all_to_all x3, waiting for transfers between devices, attention_shard(): done.append(lax.all_to_all(y, 'cp', 0, 0, tiled=True))  183 us
    all_to_all x3, waiting for transfers between devices, attention_shard(): ready.append(lax.all_to_all(packed, 'cp', 0, 0, tiled=True))  96.4 us
    pallas_call x3, Pallas kernels, pack_call(): pl.pallas_call(pack_kernel, grid=(tokens // TB,), in_specs=[big, big, sma...  28.5 us
    pallas_call x3, Pallas kernels, unpack_call(): pl.pallas_call(unpack_kernel, grid=(tokens // TB,), in_specs=[pl.BlockSpe...  25.8 us
  transfers between devices with their start and end apart: 7, of which 4 were waited for; matrix products, arithmetic and copies ran while one was open for 0% of the time, Pallas kernels for 55%

profile of v1, /device:TPU:0, one launch (start us, length us, event | category | flops | bytes accessed | tf_op | source)
XLA Modules:
  0.0 745.8 jit_solution(17298558720364715245)
XLA Ops:
  0.6 9.5 %shard_map.85 = bf16[8,384,1536]{2,1,0:T(8,128)(2,1)} custom-call(bf16[3,384,32,128]{3,2,1,0:T(8,128)(2,1)} %q_ref.5, bf16[3,384,32,128]{3,2,1,0:T(8,128)(2,1)} %g_ref.5, bf16[3,384,16,128]{3,2,1,0:T(8,128)(2,1)} %k_ref.5, bf16[3,384,16,128]{3,2,1,0:T(8,128)(2,1)} %v_ref.5), custom_call_target="tpu_custom_call" | custom-call | flops 943718400 | bytes 18874368 | tf_op jit(solution)/shard_map/pallas_call | solution.py:161
  10.1 4.3 all-to-all-start
  14.4 9.5 %shard_map.84 = bf16[8,384,1536]{2,1,0:T(8,128)(2,1)} custom-call(bf16[3,384,32,128]{3,2,1,0:T(8,128)(2,1)} %q_ref.5, bf16[3,384,32,128]{3,2,1,0:T(8,128)(2,1)} %g_ref.5, bf16[3,384,16,128]{3,2,1,0:T(8,128)(2,1)} %k_ref.5, bf16[3,384,16,128]{3,2,1,0:T(8,128)(2,1)} %v_ref.5), custom_call_target="tpu_custom_call" | custom-call | flops 943718400 | bytes 18874368 | tf_op jit(solution)/shard_map/pallas_call | solution.py:161
  23.9 96.4 %all-to-all-done = bf16[8,384,1536]{2,1,0:T(8,128)(2,1)} async-done(((bf16[8,384,1536]{2,1,0:T(8,128)(2,1)}), bf16[8,384,1536]{2,1,0:T(8,128)(2,1)}, u32[]{:S(2)}, u32[]{:S(2)}) %all-to-all-start) | async-done | bytes 9437216 | tf_op jit(solution)/shard_map/all_to_all | solution.py:220
  120.3 3.8 all-to-all-start.1
  124.1 125.6 %shard_map.88 = (bf16[3072,1536]{1,0:T(8,128)(2,1)}, f32[2,2,3072]{2,1,0:T(2,128)}) custom-call(bf16[3072,1536]{1,0:T(8,128)(2,1)} %bitcast.4.x_ref), custom_call_target="tpu_custom_call" | custom-call | flops 57982058496 | bytes 18874368 | tf_op jit(solution)/shard_map/pallas_call | solution.py:119
  249.7 3.8 all-to-all-start.3
  253.5 9.5 %shard_map.83 = bf16[8,384,1536]{2,1,0:T(8,128)(2,1)} custom-call(bf16[3,384,32,128]{3,2,1,0:T(8,128)(2,1)} %q_ref.5, bf16[3,384,32,128]{3,2,1,0:T(8,128)(2,1)} %g_ref.5, bf16[3,384,16,128]{3,2,1,0:T(8,128)(2,1)} %k_ref.5, bf16[3,384,16,128]{3,2,1,0:T(8,128)(2,1)} %v_ref.5), custom_call_target="tpu_custom_call" | custom-call | flops 943718400 | bytes 18874368 | tf_op jit(solution)/shard_map/pallas_call | solution.py:161
  263.0 95.8 %all-to-all-done.3.refs_0_ = bf16[8,384,1536]{2,1,0:T(8,128)(2,1)} async-done(((bf16[8,384,1536]{2,1,0:T(8,128)(2,1)}), bf16[8,384,1536]{2,1,0:T(8,128)(2,1)}, u32[]{:S(2)}, u32[]{:S(2)}) %all-to-all-start.3) | async-done | bytes 9437216 | tf_op jit(solution)/shard_map/all_to_all | solution.py:227
  358.8 3.8 all-to-all-start.2
  362.6 125.6 %shard_map.87 = (bf16[3072,1536]{1,0:T(8,128)(2,1)}, f32[2,2,3072]{2,1,0:T(2,128)}) custom-call(bf16[3072,1536]{1,0:T(8,128)(2,1)} %bitcast.2.x_ref), custom_call_target="tpu_custom_call" | custom-call | flops 57982058496 | bytes 18874368 | tf_op jit(solution)/shard_map/pallas_call | solution.py:119
  488.2 0.0 all-to-all-done.2
  488.2 4.0 all-to-all-start.4
  492.4 125.7 %shard_map.86 = (bf16[3072,1536]{1,0:T(8,128)(2,1)}, f32[2,2,3072]{2,1,0:T(2,128)}) custom-call(bf16[3072,1536]{1,0:T(8,128)(2,1)} %bitcast.x_ref), custom_call_target="tpu_custom_call" | custom-call | flops 57982058496 | bytes 18874368 | tf_op jit(solution)/shard_map/pallas_call | solution.py:119
  618.0 0.8 stack.14
  618.9 0.7 maximum_bitcast_fusion
  619.6 2.8 all-to-all-start.6
  622.4 5.7 all-to-all-done.6
  628.1 3.8 all-to-all-start.5
  631.9 8.6 %shard_map.89 = (bf16[3,384,32,128]{3,2,1,0:T(8,128)(2,1)}, bf16[3,384,32,128]{3,2,1,0:T(8,128)(2,1)}, bf16[3,384,16,128]{3,2,1,0:T(8,128)(2,1)}, bf16[3,384,16,128]{3,2,1,0:T(8,128)(2,1)}) custom-call(bf16[8,384,1536]{2,1,0:T(8,128)(2,1)} %all-to-all-done.3.refs_0_), custom_call_target="tpu_custom_call" | custom-call | flops 943718400 | bytes 18874368 | tf_op jit(solution)/shard_map/pallas_call | solution.py:195
  640.5 8.6 %shard_map.90 = (bf16[3,384,32,128]{3,2,1,0:T(8,128)(2,1)}, bf16[3,384,32,128]{3,2,1,0:T(8,128)(2,1)}, bf16[3,384,16,128]{3,2,1,0:T(8,128)(2,1)}, bf16[3,384,16,128]{3,2,1,0:T(8,128)(2,1)}) custom-call(bf16[8,384,1536]{2,1,0:T(8,128)(2,1)} %all-to-all-done.4.refs_0_, ...), custom_call_target="tpu_custom_call", output_to_operand_aliasing={{0}: (1, {}), {1}: (2, {}), {2}: (3, {}), {3}: (4, {})} | custom-call | flops 943718400 | bytes 18874368 | tf_op jit(solution)/shard_map/pallas_call | solution.py:195
  649.2 0.7 reshape.44
  649.9 87.3 %all-to-all-done.5.refs_0_ = bf16[8,384,1536]{2,1,0:T(8,128)(2,1)} async-done(((bf16[8,384,1536]{2,1,0:T(8,128)(2,1)}), bf16[8,384,1536]{2,1,0:T(8,128)(2,1)}, u32[]{:S(2)}, u32[]{:S(2)}) %all-to-all-start.5) | async-done | bytes 9437216 | tf_op jit(solution)/shard_map/all_to_all | solution.py:227
  737.2 8.6 %shard_map.91 = (bf16[3,384,32,128]{3,2,1,0:T(8,128)(2,1)}, bf16[3,384,32,128]{3,2,1,0:T(8,128)(2,1)}, bf16[3,384,16,128]{3,2,1,0:T(8,128)(2,1)}, bf16[3,384,16,128]{3,2,1,0:T(8,128)(2,1)}) custom-call(bf16[8,384,1536]{2,1,0:T(8,128)(2,1)} %all-to-all-done.5.refs_0_, ...), custom_call_target="tpu_custom_call", output_to_operand_aliasing={{0}: (1, {}), {1}: (2, {}), {2}: (3, {}), {3}: (4, {})} | custom-call | flops 943718400 | bytes 18874368 | tf_op jit(solution)/shard_map/pallas_call | solution.py:195
  (12 shorter events, 0.2 us)
Async XLA Ops:
  10.1 110.2 %all-to-all-start = ((bf16[8,384,1536]{2,1,0:T(8,128)(2,1)}), bf16[8,384,1536]{2,1,0:T(8,128)(2,1)}, u32[]{:S(2)}, u32[]{:S(2)}) async-start(bf16[8,384,1536]{2,1,0:T(8,128)(2,1)} %shard_map.85), calls=%async_computation | async-start | bytes 18874368 | tf_op jit(solution)/shard_map/all_to_all | solution.py:220
  120.3 129.4 %all-to-all-start.1 = ((bf16[8,384,1536]{2,1,0:T(8,128)(2,1)}), bf16[8,384,1536]{2,1,0:T(8,128)(2,1)}, u32[]{:S(2)}, u32[]{:S(2)}) async-start(bf16[8,384,1536]{2,1,0:T(8,128)(2,1)} %shard_map.84), calls=%async_computation.1 | async-start | bytes 18874368 | tf_op jit(solution)/shard_map/all_to_all | solution.py:220
  249.7 109.1 %all-to-all-start.3 = ((bf16[8,384,1536]{2,1,0:T(8,128)(2,1)}), bf16[8,384,1536]{2,1,0:T(8,128)(2,1)}, u32[]{:S(2)}, u32[]{:S(2)}) async-start(bf16[8,384,1536]{2,1,0:T(8,128)(2,1)} %bitcast.11), calls=%async_computation.3 | async-start | bytes 18874368 | tf_op jit(solution)/shard_map/all_to_all | solution.py:227
  358.8 129.5 %all-to-all-start.2 = ((bf16[8,384,1536]{2,1,0:T(8,128)(2,1)}), bf16[8,384,1536]{2,1,0:T(8,128)(2,1)}, u32[]{:S(2)}, u32[]{:S(2)}) async-start(bf16[8,384,1536]{2,1,0:T(8,128)(2,1)} %shard_map.83), calls=%async_computation.2 | async-start | bytes 18874368 | tf_op jit(solution)/shard_map/all_to_all | solution.py:220
  488.2 4.0 copy-start
  488.2 4.1 copy-start.1
  488.2 131.4 %all-to-all-start.4 = ((bf16[8,384,1536]{2,1,0:T(8,128)(2,1)}), bf16[8,384,1536]{2,1,0:T(8,128)(2,1)}, u32[]{:S(2)}, u32[]{:S(2)}) async-start(bf16[8,384,1536]{2,1,0:T(8,128)(2,1)} %bitcast.10), calls=%async_computation.4 | async-start | bytes 18874368 | tf_op jit(solution)/shard_map/all_to_all | solution.py:227
  619.6 8.5 %all-to-all-start.6 = ((f32[8,3,4,384]{3,2,1,0:T(4,128)}), f32[8,3,4,384]{3,2,1,0:T(4,128)S(1)}, u32[]{:S(2)}, u32[]{:S(2)}) async-start(f32[8,3,4,384]{3,2,1,0:T(4,128)} %maximum_bitcast_fusion), calls=%async_computation.6 | async-start | bytes 294912 | tf_op jit(solution)/shard_map/all_to_all | solution.py:233
  628.1 109.1 %all-to-all-start.5 = ((bf16[8,384,1536]{2,1,0:T(8,128)(2,1)}), bf16[8,384,1536]{2,1,0:T(8,128)(2,1)}, u32[]{:S(2)}, u32[]{:S(2)}) async-start(bf16[8,384,1536]{2,1,0:T(8,128)(2,1)} %bitcast.9), calls=%async_computation.5 | async-start | bytes 18874368 | tf_op jit(solution)/shard_map/all_to_all | solution.py:227

commit v2 on v1

--- a/solution.py
+++ b/solution.py
@@ -20,7 +20,8 @@
     return lax.dot_general(lhs, rhs, (((1,), (0,)), ((), ())), preferred_element_type=jnp.float32)
 
 
-def attention_kernel(x_ref, y_ref, lse_ref, q_cat, g_cat, k_t, v_t, s_buf, ot_acc, dqt_acc, dk_acc, dv_acc):
+def attention_kernel(x_ref, *refs):
+    y_ref, lse_ref, q_cat, g_cat, k_t, v_t, s_buf, ot_acc, dqt_acc, dk_acc, dv_acc = refs[-11:]
     seq = x_ref.shape[0]
     dim = k_t.shape[0]
     width = 2 * BQ
@@ -112,16 +113,18 @@
     lax.fori_loop(0, seq // BK, finish, 0)
 
 
-def attention_call(packed, groups, dim):
+def attention_call(packed, source, count, prev, target, total, dim):
     seq = packed.shape[0]
     wide = 6 * dim
-    pairs = groups * 2 * seq * seq // 2
+    pairs = count * seq * seq
+    operands = [packed] + ([] if prev is None else [prev])
     return pl.pallas_call(
         attention_kernel,
-        grid=(groups,),
-        in_specs=[pl.BlockSpec((seq, wide), lambda g: (0, g))],
-        out_specs=[pl.BlockSpec((seq, wide), lambda g: (0, g)), pl.BlockSpec((1, 2, seq), lambda g: (g, 0, 0))],
-        out_shape=[jax.ShapeDtypeStruct((seq, groups * wide), jnp.bfloat16), jax.ShapeDtypeStruct((groups, 2, seq), jnp.float32)],
+        grid=(count,),
+        in_specs=[pl.BlockSpec((seq, wide), lambda u: (0, source + u))] + [pl.BlockSpec(memory_space=pl.ANY)] * (len(operands) - 1),
+        out_specs=[pl.BlockSpec((seq, wide), lambda u: (0, target + u)), pl.BlockSpec((1, 2, seq), lambda u: (u, 0, 0))],
+        out_shape=[jax.ShapeDtypeStruct((seq, total * wide), jnp.bfloat16), jax.ShapeDtypeStruct((count, 2, seq), jnp.float32)],
+        input_output_aliases={1: 0} if prev is not None else {},
         scratch_shapes=[
             pltpu.VMEM((2 * BQ, dim), jnp.bfloat16),
             pltpu.VMEM((2 * BQ, dim), jnp.bfloat16),
@@ -133,105 +136,114 @@
             pltpu.VMEM((seq, dim), jnp.float32),
             pltpu.VMEM((seq, dim), jnp.float32),
         ],
-        compiler_params=pltpu.CompilerParams(dimension_semantics=("arbitrary",), vmem_limit_bytes=60 * 1024 * 1024),
-        cost_estimate=pl.CostEstimate(flops=pairs * dim * 2 * 12, bytes_accessed=packed.size * 4, transcendentals=pairs * 2),
-    )(packed)
+        compiler_params=pltpu.CompilerParams(dimension_semantics=("arbitrary",), vmem_limit_bytes=62 * 1024 * 1024),
+        cost_estimate=pl.CostEstimate(flops=pairs * dim * 12, bytes_accessed=count * seq * wide * 4, transcendentals=pairs * 2),
+    )(*operands)
 
 
 def pack_kernel(q_ref, g_ref, k_ref, v_ref, o_ref):
-    parts, _ = o_ref.shape[:2]
     dim = q_ref.shape[-1]
-    groups = k_ref.shape[2] // parts
-    wide = 6 * dim
     for ref, first, count in ((q_ref, 0, 2), (g_ref, 2, 2), (k_ref, 4, 1), (v_ref, 5, 1)):
         by_head = pltpu.einshape("thd->htd", ref[0])
         for head in range(ref.shape[2]):
-            part, local = divmod(head, groups * count)
-            group, lane = divmod(local, count)
-            start = group * wide + (first + lane) * dim
+            part, lane = divmod(head, count)
+            start = (first + lane) * dim
             o_ref[part, :, start:start + dim] = by_head[head]
 
 
-def pack_call(queries, out_grad, keys, values, idx, parts):
-    _, tokens, heads, dim = queries.shape
-    kv_heads = keys.shape[2]
-    width = kv_heads // parts * 6 * dim
-    big = pl.BlockSpec((1, TB, heads, dim), lambda i: (idx, i, 0, 0))
-    small = pl.BlockSpec((1, TB, kv_heads, dim), lambda i: (idx, i, 0, 0))
+def unit_specs(first, parts, dim):
+    def spec(count):
+        return pl.BlockSpec((1, TB, parts * count, dim), lambda u, i: ((first + u) // 2, i, (first + u) % 2, 0))
+
+    return spec(2), spec(1), pl.BlockSpec((parts, TB, 6 * dim), lambda u, i: (0, i, u))
+
+
+def pack_call(queries, out_grad, keys, values, first, count, parts):
+    tokens, dim = queries.shape[1], queries.shape[3]
+    big, small, packed = unit_specs(first, parts, dim)
+    size = parts * tokens * count * 6 * dim
     return pl.pallas_call(
         pack_kernel,
-        grid=(tokens // TB,),
+        grid=(count, tokens // TB),
         in_specs=[big, big, small, small],
-        out_specs=pl.BlockSpec((parts, TB, width), lambda i: (0, i, 0)),
-        out_shape=jax.ShapeDtypeStruct((parts, tokens, width), jnp.bfloat16),
-        compiler_params=pltpu.CompilerParams(dimension_semantics=("arbitrary",), vmem_limit_bytes=62 * 1024 * 1024),
-        cost_estimate=pl.CostEstimate(flops=parts * tokens * width * 200, bytes_accessed=parts * tokens * width * 4, transcendentals=0),
+        out_specs=packed,
+        out_shape=jax.ShapeDtypeStruct((parts, tokens, count * 6 * dim), jnp.bfloat16),
+        compiler_params=pltpu.CompilerParams(dimension_semantics=("arbitrary", "arbitrary"), vmem_limit_bytes=62 * 1024 * 1024),
+        cost_estimate=pl.CostEstimate(flops=size * 200, bytes_accessed=size * 4, transcendentals=0),
     )(queries, out_grad, keys, values)
 
 
 def unpack_kernel(*refs):
     y_ref = refs[0]
     o_ref, dq_ref, dk_ref, dv_ref = refs[-4:]
-    parts = y_ref.shape[0]
     dim = o_ref.shape[-1]
-    groups = dk_ref.shape[2] // parts
-    wide = 6 * dim
     for ref, first, count in ((o_ref, 0, 2), (dq_ref, 2, 2), (dk_ref, 4, 1), (dv_ref, 5, 1)):
         rows = []
         for head in range(ref.shape[2]):
-            part, local = divmod(head, groups * count)
-            group, lane = divmod(local, count)
-            start = group * wide + (first + lane) * dim
+            part, lane = divmod(head, count)
+            start = (first + lane) * dim
             rows.append(y_ref[part, :, start:start + dim])
         ref[0] = pltpu.einshape("htd->thd", jnp.stack(rows))
 
 
-def unpack_call(y, prev, idx, batch, heads, kv_heads, dim):
-    parts, tokens, width = y.shape
-    big = pl.BlockSpec((1, TB, heads, dim), lambda i: (idx, i, 0, 0))
-    small = pl.BlockSpec((1, TB, kv_heads, dim), lambda i: (idx, i, 0, 0))
-    big_shape = jax.ShapeDtypeStruct((batch, tokens, heads, dim), jnp.bfloat16)
-    small_shape = jax.ShapeDtypeStruct((batch, tokens, kv_heads, dim), jnp.bfloat16)
+def unpack_call(y, prev, first, count, shapes):
+    parts, tokens = y.shape[:2]
+    dim = shapes[0].shape[3]
+    big, small, packed = unit_specs(first, parts, dim)
     return pl.pallas_call(
         unpack_kernel,
-        grid=(tokens // TB,),
-        in_specs=[pl.BlockSpec((parts, TB, width), lambda i: (0, i, 0))] + [pl.BlockSpec(memory_space=pl.ANY)] * len(prev),
+        grid=(count, tokens // TB),
+        in_specs=[packed] + [pl.BlockSpec(memory_space=pl.ANY)] * len(prev),
         out_specs=[big, big, small, small],
-        out_shape=[big_shape, big_shape, small_shape, small_shape],
+        out_shape=shapes,
         input_output_aliases={i + 1: i for i in range(len(prev))},
-        compiler_params=pltpu.CompilerParams(dimension_semantics=("arbitrary",), vmem_limit_bytes=62 * 1024 * 1024),
+        compiler_params=pltpu.CompilerParams(dimension_semantics=("arbitrary", "arbitrary"), vmem_limit_bytes=62 * 1024 * 1024),
         cost_estimate=pl.CostEstimate(flops=y.size * 200, bytes_accessed=y.size * 4, transcendentals=0),
     )(y, *prev)
 
 
+IN_UNITS = ((0, 1), (1, 2), (3, 3))
+OUT_UNITS = ((0, 3), (3, 2), (5, 1))
+RUNS = ((0, 1), (1, 2), (3, 2), (5, 1))
+
+
+def holder(units, unit):
+    return next(idx for idx, (first, count) in enumerate(units) if first <= unit < first + count)
+
+
 def solution(mesh):
     cp_size = mesh.shape["cp"]
 
     def attention_shard(queries, keys, values, out_grad):
         batch, tokens, heads, dim = queries.shape
-        kv_heads = keys.shape[2]
-        groups = kv_heads // cp_size
-        width = groups * 6 * dim
-        ready, sums = [], []
-        for idx in range(batch):
-            packed = pack_call(queries, out_grad, keys, values, idx, cp_size)
+        seq = cp_size * tokens
+        ready = []
+        for idx, (first, count) in enumerate(IN_UNITS):
+            packed = pack_call(queries, out_grad, keys, values, first, count, cp_size)
             if idx:
                 packed, ready[-1] = lax.optimization_barrier((packed, ready[-1]))
             ready.append(lax.all_to_all(packed, "cp", 0, 0, tiled=True))
+        results, sums = {}, []
+        for first, count in RUNS:
+            src, dst = holder(IN_UNITS, first), holder(OUT_UNITS, first)
+            results[dst], lse = attention_call(
+                ready[src].reshape(seq, -1), first - IN_UNITS[src][0], count,
+                results.get(dst), first - OUT_UNITS[dst][0], OUT_UNITS[dst][1], dim)
+            sums.append(lse)
         done = []
-        for idx in range(batch):
-            y, lse = attention_call(ready[idx].reshape(cp_size * tokens, width), groups, dim)
-            y = y.reshape(cp_size, tokens, width)
+        for idx in range(len(OUT_UNITS)):
+            y = results[idx].reshape(cp_size, tokens, -1)
             if idx:
                 y, done[-1] = lax.optimization_barrier((y, done[-1]))
             done.append(lax.all_to_all(y, "cp", 0, 0, tiled=True))
-            sums.append(lse)
+        big = jax.ShapeDtypeStruct(queries.shape, jnp.bfloat16)
+        small = jax.ShapeDtypeStruct(keys.shape, jnp.bfloat16)
         outs = ()
-        for idx in range(batch):
-            outs = unpack_call(done[idx], outs, idx, batch, heads, kv_heads, dim)
-        lse = jnp.stack(sums).reshape(batch, groups * 2, cp_size, tokens)
-        lse = lax.all_to_all(jnp.transpose(lse, (2, 0, 1, 3)), "cp", 0, 0, tiled=True)
-        lse = jnp.transpose(lse, (1, 0, 2, 3)).reshape(batch, heads, tokens)
+        for idx, (first, count) in enumerate(OUT_UNITS):
+            outs = unpack_call(done[idx], outs, first, count, (big, big, small, small))
+        lse = jnp.concatenate(sums).reshape(batch, 2, 2, cp_size, tokens)
+        lse = lax.all_to_all(jnp.transpose(lse, (3, 0, 1, 2, 4)), "cp", 0, 0, tiled=True)
+        lse = jnp.transpose(lse, (1, 2, 0, 3, 4)).reshape(batch, heads, tokens)
         return outs[0], lse, outs[1], outs[2], outs[3]
 
     seq_spec = P("dp", "cp")

time: 747 us -> 714 us (0.956)
  waiting for transfers between devices: 285 us -> 228 us
  Pallas kernels: 431 us -> 455 us
    all_to_all x3, waiting for transfers between devices: 183 us -> 91.9 us  [attention_shard(): done.append(lax.all_to_all(y, 'cp', 0, 0, tiled=True))]
    all_to_all x3, waiting for transfers between devices: 96.4 us -> 130 us  [attention_shard(): ready.append(lax.all_to_all(packed, 'cp', 0, 0, tiled=True))]
    pallas_call x9 -> x10, Pallas kernels: 431 us -> 455 us  [the longest x4 381 us: attention_call(): pl.pallas_call(attention_kernel, grid=(count,), in_specs=[pl.BlockSpec((s...]
  transfers between devices with their start and end apart: 7 -> 7, of which waited for: 4 -> 6; matrix products, arithmetic and copies ran while one was open for 0% -> 0% of each run, Pallas kernels for 55% -> 62%
where the time goes in v2:
time: 714 us; the launch traced here: 711 us
  Pallas kernels  455 us (64%)
  waiting for transfers between devices  228 us (32%)
  starting transfers between devices  25.8 us (4%)
    pallas_call x4, Pallas kernels, attention_call(): pl.pallas_call(attention_kernel, grid=(count,), in_specs=[pl.BlockSpec((s...  381 us
    all_to_all x3, waiting for transfers between devices, attention_shard(): ready.append(lax.all_to_all(packed, 'cp', 0, 0, tiled=True))  130 us
    all_to_all x3, waiting for transfers between devices, attention_shard(): done.append(lax.all_to_all(y, 'cp', 0, 0, tiled=True))  91.9 us
    pallas_call x3, Pallas kernels, unpack_call(): pl.pallas_call(unpack_kernel, grid=(count, tokens // TB), in_specs=[packe...  37.4 us
    pallas_call x3, Pallas kernels, pack_call(): pl.pallas_call(pack_kernel, grid=(count, tokens // TB), in_specs=[big, bi...  36.3 us
  transfers between devices with their start and end apart: 7, of which 6 were waited for; matrix products, arithmetic and copies ran while one was open for 0% of the time, Pallas kernels for 62%

profile of v2, /device:TPU:0, one launch (start us, length us, event | category | flops | bytes accessed | tf_op | source)
XLA Modules:
  0.0 711.5 jit_solution(12346513969069377293)
XLA Ops:
  0.6 6.4 shard_map.85
  7.0 4.3 all-to-all-start
  11.3 12.2 %shard_map.84 = bf16[8,384,1536]{2,1,0:T(8,128)(2,1)} custom-call(bf16[3,384,32,128]{3,2,1,0:T(8,128)(2,1)} %q_ref.5, bf16[3,384,32,128]{3,2,1,0:T(8,128)(2,1)} %g_ref.5, bf16[3,384,16,128]{3,2,1,0:T(8,128)(2,1)} %k_ref.5, bf16[3,384,16,128]{3,2,1,0:T(8,128)(2,1)} %v_ref.5), custom_call_target="tpu_custom_call" | custom-call | flops 943718400 | bytes 18874368 | tf_op jit(solution)/shard_map/pallas_call | solution.py:165
  23.5 42.6 %all-to-all-done = bf16[8,384,768]{2,1,0:T(8,128)(2,1)} async-done(((bf16[8,384,768]{2,1,0:T(8,128)(2,1)}), bf16[8,384,768]{2,1,0:T(8,128)(2,1)}, u32[]{:S(2)}, u32[]{:S(2)}) %all-to-all-start) | async-done | bytes 4718624 | tf_op jit(solution)/shard_map/all_to_all | solution.py:225
  66.1 3.8 all-to-all-start.1
  70.0 17.7 %shard_map.83 = bf16[8,384,2304]{2,1,0:T(8,128)(2,1)} custom-call(bf16[3,384,32,128]{3,2,1,0:T(8,128)(2,1)} %q_ref.5, bf16[3,384,32,128]{3,2,1,0:T(8,128)(2,1)} %g_ref.5, bf16[3,384,16,128]{3,2,1,0:T(8,128)(2,1)} %k_ref.5, bf16[3,384,16,128]{3,2,1,0:T(8,128)(2,1)} %v_ref.5), custom_call_target="tpu_custom_call" | custom-call | flops 1415577600 | bytes 28311552 | tf_op jit(solution)/shard_map/pallas_call | solution.py:165
  87.6 87.6 %all-to-all-done.1 = bf16[8,384,1536]{2,1,0:T(8,128)(2,1)} async-done(((bf16[8,384,1536]{2,1,0:T(8,128)(2,1)}), bf16[8,384,1536]{2,1,0:T(8,128)(2,1)}, u32[]{:S(2)}, u32[]{:S(2)}) %all-to-all-start.1) | async-done | bytes 9437216 | tf_op jit(solution)/shard_map/all_to_all | solution.py:225
  175.3 4.2 all-to-all-start.2
  179.5 65.0 %shard_map.88 = (bf16[3072,2304]{1,0:T(8,128)(2,1)}, f32[1,2,3072]{2,1,0:T(2,128)}) custom-call(bf16[3072,768]{1,0:T(8,128)(2,1)} %bitcast.4.x_ref), custom_call_target="tpu_custom_call" | custom-call | flops 14495514624 | bytes 9437184 | tf_op jit(solution)/shard_map/pallas_call | solution.py:121
  244.5 125.5 %shard_map.89 = (bf16[3072,2304]{1,0:T(8,128)(2,1)}, f32[2,2,3072]{2,1,0:T(2,128)}) custom-call(bf16[3072,1536]{1,0:T(8,128)(2,1)} %bitcast.3.x_ref, bf16[3072,2304]{1,0:T(8,128)(2,1)} %get-tuple-element.39.refs_0_), custom_call_target="tpu_custom_call", output_to_operand_aliasing={{0}: (1, {})} | custom-call | flops 28991029248 | bytes 18874368 | tf_op jit(solution)/shard_map/pallas_call | solution.py:121
  370.0 4.2 all-to-all-start.3
  374.2 125.6 %shard_map.87 = (bf16[3072,1536]{1,0:T(8,128)(2,1)}, f32[2,2,3072]{2,1,0:T(2,128)}) custom-call(bf16[3072,2304]{1,0:T(8,128)(2,1)} %bitcast.x_ref), custom_call_target="tpu_custom_call" | custom-call | flops 28991029248 | bytes 18874368 | tf_op jit(solution)/shard_map/pallas_call | solution.py:121
  499.8 30.3 %all-to-all-done.3.refs_0_ = bf16[8,384,2304]{2,1,0:T(8,128)(2,1)} async-done(((bf16[8,384,2304]{2,1,0:T(8,128)(2,1)}), bf16[8,384,2304]{2,1,0:T(8,128)(2,1)}, u32[]{:S(2)}, u32[]{:S(2)}) %all-to-all-start.3) | async-done | bytes 14155808 | tf_op jit(solution)/shard_map/all_to_all | solution.py:238
  530.1 3.8 all-to-all-start.4
  533.9 64.9 %shard_map.86 = (bf16[3072,768]{1,0:T(8,128)(2,1)}, f32[1,2,3072]{2,1,0:T(2,128)}) custom-call(bf16[3072,2304]{1,0:T(8,128)(2,1)} %bitcast.x_ref), custom_call_target="tpu_custom_call" | custom-call | flops 14495514624 | bytes 9437184 | tf_op jit(solution)/shard_map/pallas_call | solution.py:121
  598.9 0.8 pad_maximum_fusion
  600.6 38.6 %all-to-all-done.4.refs_0_ = bf16[8,384,1536]{2,1,0:T(8,128)(2,1)} async-done(((bf16[8,384,1536]{2,1,0:T(8,128)(2,1)}), bf16[8,384,1536]{2,1,0:T(8,128)(2,1)}, u32[]{:S(2)}, u32[]{:S(2)}) %all-to-all-start.4) | async-done | bytes 9437216 | tf_op jit(solution)/shard_map/all_to_all | solution.py:238
  639.2 2.1 all-to-all-start.6
  641.3 5.6 all-to-all-done.6
  646.9 3.3 all-to-all-start.5
  650.3 18.4 %shard_map.90 = (bf16[3,384,32,128]{3,2,1,0:T(8,128)(2,1)}, bf16[3,384,32,128]{3,2,1,0:T(8,128)(2,1)}, bf16[3,384,16,128]{3,2,1,0:T(8,128)(2,1)}, bf16[3,384,16,128]{3,2,1,0:T(8,128)(2,1)}) custom-call(bf16[8,384,2304]{2,1,0:T(8,128)(2,1)} %all-to-all-done.3.refs_0_), custom_call_target="tpu_custom_call" | custom-call | flops 1415577600 | bytes 28311552 | tf_op jit(solution)/shard_map/pallas_call | solution.py:193
  669.5 12.5 %shard_map.91 = (bf16[3,384,32,128]{3,2,1,0:T(8,128)(2,1)}, bf16[3,384,32,128]{3,2,1,0:T(8,128)(2,1)}, bf16[3,384,16,128]{3,2,1,0:T(8,128)(2,1)}, bf16[3,384,16,128]{3,2,1,0:T(8,128)(2,1)}) custom-call(bf16[8,384,1536]{2,1,0:T(8,128)(2,1)} %all-to-all-done.4.refs_0_, ...), custom_call_target="tpu_custom_call", output_to_operand_aliasing={{0}: (1, {}), {1}: (2, {}), {2}: (3, {}), {3}: (4, {})} | custom-call | flops 943718400 | bytes 18874368 | tf_op jit(solution)/shard_map/pallas_call | solution.py:193
  682.0 23.0 %all-to-all-done.5.refs_0_ = bf16[8,384,768]{2,1,0:T(8,128)(2,1)} async-done(((bf16[8,384,768]{2,1,0:T(8,128)(2,1)}), bf16[8,384,768]{2,1,0:T(8,128)(2,1)}, u32[]{:S(2)}, u32[]{:S(2)}) %all-to-all-start.5) | async-done | bytes 4718624 | tf_op jit(solution)/shard_map/all_to_all | solution.py:238
  705.0 6.5 shard_map.92
  (11 shorter events, 1.7 us)
Async XLA Ops:
  7.0 59.1 %all-to-all-start = ((bf16[8,384,768]{2,1,0:T(8,128)(2,1)}), bf16[8,384,768]{2,1,0:T(8,128)(2,1)}, u32[]{:S(2)}, u32[]{:S(2)}) async-start(bf16[8,384,768]{2,1,0:T(8,128)(2,1)} %shard_map.85), calls=%async_computation | async-start | bytes 9437184 | tf_op jit(solution)/shard_map/all_to_all | solution.py:225
  66.1 109.1 %all-to-all-start.1 = ((bf16[8,384,1536]{2,1,0:T(8,128)(2,1)}), bf16[8,384,1536]{2,1,0:T(8,128)(2,1)}, u32[]{:S(2)}, u32[]{:S(2)}) async-start(bf16[8,384,1536]{2,1,0:T(8,128)(2,1)} %shard_map.84), calls=%async_computation.1 | async-start | bytes 18874368 | tf_op jit(solution)/shard_map/all_to_all | solution.py:225
  175.3 194.8 %all-to-all-start.2 = ((bf16[8,384,2304]{2,1,0:T(8,128)(2,1)}), bf16[8,384,2304]{2,1,0:T(8,128)(2,1)}, u32[]{:S(2)}, u32[]{:S(2)}) async-start(bf16[8,384,2304]{2,1,0:T(8,128)(2,1)} %shard_map.83), calls=%async_computation.2 | async-start | bytes 28311552 | tf_op jit(solution)/shard_map/all_to_all | solution.py:225
  370.0 160.1 %all-to-all-start.3 = ((bf16[8,384,2304]{2,1,0:T(8,128)(2,1)}), bf16[8,384,2304]{2,1,0:T(8,128)(2,1)}, u32[]{:S(2)}, u32[]{:S(2)}) async-start(bf16[8,384,2304]{2,1,0:T(8,128)(2,1)} %bitcast.10), calls=%async_computation.3 | async-start | bytes 28311552 | tf_op jit(solution)/shard_map/all_to_all | solution.py:238
  530.1 109.1 %all-to-all-start.4 = ((bf16[8,384,1536]{2,1,0:T(8,128)(2,1)}), bf16[8,384,1536]{2,1,0:T(8,128)(2,1)}, u32[]{:S(2)}, u32[]{:S(2)}) async-start(bf16[8,384,1536]{2,1,0:T(8,128)(2,1)} %bitcast.11), calls=%async_computation.4 | async-start | bytes 18874368 | tf_op jit(solution)/shard_map/all_to_all | solution.py:238
  533.9 65.0 %copy-start = (f32[2,2,3072]{2,1,0:T(2,128)S(1)}, f32[2,2,3072]{2,1,0:T(2,128)}, u32[]{:S(2)}) copy-start(f32[2,2,3072]{2,1,0:T(2,128)} %get-tuple-element.55) | copy-start | bytes 147460
  533.9 65.0 %copy-start.1 = (f32[2,2,3072]{2,1,0:T(2,128)S(1)}, f32[2,2,3072]{2,1,0:T(2,128)}, u32[]{:S(2)}) copy-start(f32[2,2,3072]{2,1,0:T(2,128)} %get-tuple-element.56) | copy-start | bytes 147460
  533.9 65.0 %copy-start.2 = (f32[1,2,3072]{2,1,0:T(2,128)S(1)}, f32[1,2,3072]{2,1,0:T(2,128)}, u32[]{:S(2)}) copy-start(f32[1,2,3072]{2,1,0:T(2,128)} %get-tuple-element.54) | copy-start | bytes 73732
  639.2 7.7 %all-to-all-start.6 = ((f32[8,3,2,2,384]{4,3,2,1,0:T(2,128)}), f32[8,3,2,2,384]{4,3,2,1,0:T(2,128)S(1)}, u32[]{:S(2)}, u32[]{:S(2)}) async-start(f32[8,3,2,2,384]{4,3,2,1,0:T(2,128)} %bitcast.9), calls=%async_computation.6 | async-start | bytes 294912 | tf_op jit(solution)/shard_map/all_to_all | solution.py:245
  646.9 58.1 %all-to-all-start.5 = ((bf16[8,384,768]{2,1,0:T(8,128)(2,1)}), bf16[8,384,768]{2,1,0:T(8,128)(2,1)}, u32[]{:S(2)}, u32[]{:S(2)}) async-start(bf16[8,384,768]{2,1,0:T(8,128)(2,1)} %bitcast.12), calls=%async_computation.5 | async-start | bytes 9437184 | tf_op jit(solution)/shard_map/all_to_all | solution.py:238

commit v3 on v2

v3 whole, which is shorter than its diff:
```python
import functools

import jax
import jax.numpy as jnp
from jax import lax
from jax.experimental import pallas as pl
from jax.experimental.pallas import tpu as pltpu
from jax.sharding import PartitionSpec as P


LOG2E = 1.4426950408889634
BQ = 256
BK = 512
TB = 64


def dot_nt(lhs, rhs):
    return lax.dot_general(lhs, rhs, (((1,), (1,)), ((), ())), preferred_element_type=jnp.float32)


def dot_nn(lhs, rhs):
    return lax.dot_general(lhs, rhs, (((1,), (0,)), ((), ())), preferred_element_type=jnp.float32)


def attention_kernel(x_ref, *refs):
    y_ref, lse_ref, q_cat, g_cat, k_t, v_t, s_even, s_odd, ot_acc, dqt_acc, dk_acc, dv_acc = refs[-12:]
    seq = x_ref.shape[0]
    dim = k_t.shape[0]
    width = 2 * BQ
    scale = dim ** -0.5
    scale2 = scale * LOG2E
    q_col, g_col, k_col, v_col = 0, 2 * dim, 4 * dim, 5 * dim

    def prepare(blk, carry):
        rows = pl.ds(pl.multiple_of(blk * BK, BK), BK)
        k_t[:, rows] = x_ref[rows, k_col:k_col + dim].T
        v_t[:, rows] = x_ref[rows, v_col:v_col + dim].T
        dk_acc[rows, :] = jnp.zeros((BK, dim), jnp.float32)
        dv_acc[rows, :] = jnp.zeros((BK, dim), jnp.float32)
        return carry

    lax.fori_loop(0, seq // BK, prepare, 0)

    def fold(tile, op):
        return op(tile.reshape(BK // 8, 8, width), axis=0)

    def query_block(blk, carry):
        rows = pl.ds(pl.multiple_of(blk * BQ, BQ), BQ)
        for head in range(2):
            q_cat[head * BQ:(head + 1) * BQ, :] = x_ref[rows, q_col + head * dim:q_col + (head + 1) * dim]
            g_cat[head * BQ:(head + 1) * BQ, :] = x_ref[rows, g_col + head * dim:g_col + (head + 1) * dim]
        last = (blk * BQ) // BK

        def key_rows(step):
            return pl.ds(pl.multiple_of(step * BK, BK), BK)

        def slot(idx):
            return pl.ds(pl.multiple_of(idx * BK, BK), BK)

        def absorb(src, idx, step, carry):
            acc_max, run_max, run_sum = carry
            alpha = jnp.exp2((acc_max - run_max) * scale2)
            weights = jnp.exp2(src[slot(idx), :] * scale2 - run_max * scale2)
            ot_acc[...] = ot_acc[...] * alpha + dot_nn(v_t[:, key_rows(step)], weights.astype(jnp.bfloat16))
            return run_sum * alpha + fold(weights, jnp.sum)

        def advance(dst, idx, step, src, src_idx, src_step, carry):
            scores = dot_nt(x_ref[key_rows(step), k_col:k_col + dim], q_cat[...])
            dst[slot(idx), :] = scores
            new_max = jnp.maximum(carry[1], jnp.max(fold(scores, jnp.max), axis=0, keepdims=True))
            run_sum = absorb(src, src_idx, src_step, carry)
            return carry[1], new_max, run_sum

        def before(pair):
            return jnp.where(pair == 0, last, 2 * pair - 1)

        def score_pair(pair, carry):
            carry = advance(s_even, pair, 2 * pair, s_odd, pair, before(pair), carry)
            return advance(s_odd, pair + 1, 2 * pair + 1, s_even, pair, 2 * pair, carry)

        half = last // 2

        def finish_even(carry):
            carry = advance(s_even, half, 2 * half, s_odd, half, before(half), carry)
            return carry[1], absorb(s_even, half, 2 * half, carry)

        def finish_odd(carry):
            return carry[1], absorb(s_odd, half, before(half), carry)

        scores = dot_nt(x_ref[key_rows(last), k_col:k_col + dim], q_cat[...])
        key_pos = last * BK + lax.broadcasted_iota(jnp.int32, (BK, width), 0)
        query_pos = blk * BQ + lax.broadcasted_iota(jnp.int32, (BK, width), 1) % BQ
        scores = jnp.where(key_pos <= query_pos, scores, -jnp.inf)
        s_odd[slot(0), :] = scores
        row_max = jnp.max(fold(scores, jnp.max), axis=0, keepdims=True)
        ot_acc[...] = jnp.zeros_like(ot_acc)
        state = lax.fori_loop(0, half, score_pair, (row_max, row_max, jnp.zeros((8, width), jnp.float32)))
        row_max, run_sum = lax.cond(last % 2 == 1, finish_even, finish_odd, state)
        row_sum = jnp.sum(run_sum, axis=0, keepdims=True)
        out_t = (ot_acc[...] / row_sum).astype(jnp.bfloat16)
        row_lse = row_max * scale + jnp.log(row_sum)
        lse2 = row_lse * LOG2E
        out_f = out_t.astype(jnp.float32)
        grad_t = g_cat[...].astype(jnp.float32).T
        delta = jnp.sum(out_f * grad_t, axis=0, keepdims=True)
        out_n = out_f.T.astype(jnp.bfloat16)
        for head in range(2):
            y_ref[rows, head * dim:(head + 1) * dim] = out_n[head * BQ:(head + 1) * BQ, :]
            lse_ref[0, head:head + 1, rows] = row_lse[:, head * BQ:(head + 1) * BQ]
        dqt_acc[...] = jnp.zeros_like(dqt_acc)

        def grad_step(src, idx, step):
            probs = jnp.exp2(src[slot(idx), :] * scale2 - lse2)
            grad_prob = dot_nt(x_ref[key_rows(step), v_col:v_col + dim], g_cat[...])
            grad_score = (probs * (grad_prob - delta)).astype(jnp.bfloat16)
            dv_acc[key_rows(step), :] += dot_nn(probs.astype(jnp.bfloat16), g_cat[...])
            dk_acc[key_rows(step), :] += dot_nn(grad_score, q_cat[...])
            dqt_acc[...] += dot_nn(k_t[:, key_rows(step)], grad_score)

        def grad_pair(pair, inner):
            grad_step(s_odd, pair, before(pair))
            grad_step(s_even, pair, 2 * pair)
            return inner

        lax.fori_loop(0, (last + 1) // 2, grad_pair, 0)

        @pl.when(last % 2 == 0)
        def _():
            grad_step(s_odd, half, before(half))

        dq_n = (dqt_acc[...] * scale).T.astype(jnp.bfloat16)
        for head in range(2):
            y_ref[rows, (2 + head) * dim:(3 + head) * dim] = dq_n[head * BQ:(head + 1) * BQ, :]
        return carry

    lax.fori_loop(0, seq // BQ, query_block, 0)

    def finish(blk, carry):
        rows = pl.ds(pl.multiple_of(blk * BK, BK), BK)
        y_ref[rows, 4 * dim:5 * dim] = (dk_acc[rows, :] * scale).astype(jnp.bfloat16)
        y_ref[rows, 5 * dim:6 * dim] = dv_acc[rows, :].astype(jnp.bfloat16)
        return carry

    lax.fori_loop(0, seq // BK, finish, 0)


def attention_scratch(seq, dim):
    return [
        pltpu.VMEM((2 * BQ, dim), jnp.bfloat16),
        pltpu.VMEM((2 * BQ, dim), jnp.bfloat16),
        pltpu.VMEM((dim, seq), jnp.bfloat16),
        pltpu.VMEM((dim, seq), jnp.bfloat16),
        pltpu.VMEM((seq // 2, 2 * BQ), jnp.float32),
        pltpu.VMEM((seq // 2, 2 * BQ), jnp.float32),
        pltpu.VMEM((dim, 2 * BQ), jnp.float32),
        pltpu.VMEM((dim, 2 * BQ), jnp.float32),
        pltpu.VMEM((seq, dim), jnp.float32),
        pltpu.VMEM((seq, dim), jnp.float32),
    ]


def pack_kernel(q_ref, g_ref, k_ref, v_ref, o_ref):
    dim = q_ref.shape[-1]
    for ref, first, count in ((q_ref, 0, 2), (g_ref, 2, 2), (k_ref, 4, 1), (v_ref, 5, 1)):
        by_head = pltpu.einshape("thd->htd", ref[0])
        for head in range(ref.shape[2]):
            part, lane = divmod(head, count)
            start = (first + lane) * dim
            o_ref[part, :, start:start + dim] = by_head[head]


def unit_specs(first, parts, dim, skip=0):
    def spec(count):
        return pl.BlockSpec((1, TB, parts * count, dim), lambda u, i: ((first + u) // 2, skip + i, (first + u) % 2, 0))

    return spec(2), spec(1), pl.BlockSpec((parts, TB, 6 * dim), lambda u, i: (0, i, u))


def unpack_kernel(*refs):
    y_ref = refs[0]
    o_ref, dq_ref, dk_ref, dv_ref = refs[-4:]
    dim = o_ref.shape[-1]
    for ref, first, count in ((o_ref, 0, 2), (dq_ref, 2, 2), (dk_ref, 4, 1), (dv_ref, 5, 1)):
        rows = []
        for head in range(ref.shape[2]):
            part, lane = divmod(head, count)
            start = (first + lane) * dim
            rows.append(y_ref[part, :, start:start + dim])
        ref[0] = pltpu.einshape("htd->thd", jnp.stack(rows))


def peer_rows(offset, tokens, piece=0, pieces=1):
    size = tokens // pieces
    start = jnp.bitwise_xor(lax.axis_index("cp"), offset) * tokens + piece * size
    return pl.ds(pl.multiple_of(start, size), size)


def attention_split_kernel(split_in, split_out, parts, *refs):
    count_in, count_out = (parts if split_in else 1), parts * split_out
    ins, outs, lse_ref = refs[:count_in], refs[count_in:count_in + count_out], refs[count_in + count_out]
    scratch = refs[count_in + count_out + 1:]
    x_ref, y_ref, sems = scratch[-3:]
    tokens = x_ref.shape[0] // parts
    if split_in:
        copies = [pltpu.make_async_copy(ref, x_ref.at[peer_rows(k, tokens)], sems.at[k]) for k, ref in enumerate(ins)]
    else:
        copies = [pltpu.make_async_copy(ins[0], x_ref, sems.at[0])]
    for copy in copies:
        copy.start()
    for copy in copies:
        copy.wait()
    attention_kernel(x_ref, y_ref, lse_ref, *scratch[:-3])
    copies = [
        pltpu.make_async_copy(y_ref.at[peer_rows(idx % parts, tokens, idx // parts, split_out)], ref, sems.at[idx])
        for idx, ref in enumerate(outs)
    ]
    for copy in copies:
        copy.start()
    for copy in copies:
        copy.wait()


def attention_split_call(ins, split_out, parts, seq, dim):
    wide = 6 * dim
    split_in = len(ins) > 1
    pairs = seq * seq
    any_spec = pl.BlockSpec(memory_space=pl.ANY)
    y_shapes = [jax.ShapeDtypeStruct((seq // parts // split_out, wide), jnp.bfloat16)] * (parts * split_out)
    res = pl.pallas_call(
        functools.partial(attention_split_kernel, split_in, split_out, parts),
        in_specs=[any_spec] * len(ins),
        out_specs=[any_spec] * len(y_shapes) + [pl.BlockSpec(memory_space=pltpu.VMEM)],
        out_shape=y_shapes + [jax.ShapeDtypeStruct((1, 2, seq), jnp.float32)],
        scratch_shapes=attention_scratch(seq, dim) + [
            pltpu.VMEM((seq, wide), jnp.bfloat16),
            pltpu.VMEM((seq, wide), jnp.bfloat16),
            pltpu.SemaphoreType.DMA((2 * parts,)),
        ],
        compiler_params=pltpu.CompilerParams(vmem_limit_bytes=62 * 1024 * 1024),
        cost_estimate=pl.CostEstimate(flops=pairs * dim * 12, bytes_accessed=seq * wide * 4, transcendentals=pairs * 2),
    )(*ins)
    return res[:-1], res[-1]


def pack_split_kernel(q_ref, g_ref, k_ref, v_ref, *refs):
    *outs, buf = refs
    pack_kernel(q_ref, g_ref, k_ref, v_ref, buf)
    for k, ref in enumerate(outs):
        ref[...] = buf[jnp.bitwise_xor(lax.axis_index("cp"), k)]


def pack_split_call(queries, out_grad, keys, values, unit, parts):
    tokens, dim = queries.shape[1], queries.shape[3]
    big, small, _ = unit_specs(unit, parts, dim)
    wide = 6 * dim
    size = parts * tokens * wide
    return pl.pallas_call(
        pack_split_kernel,
        grid=(1, tokens // TB),
        in_specs=[big, big, small, small],
        out_specs=[pl.BlockSpec((TB, wide), lambda u, i: (i, 0))] * parts,
        out_shape=[jax.ShapeDtypeStruct((tokens, wide), jnp.bfloat16)] * parts,
        scratch_shapes=[pltpu.VMEM((parts, TB, wide), jnp.bfloat16)],
        compiler_params=pltpu.CompilerParams(dimension_semantics=("arbitrary", "arbitrary"), vmem_limit_bytes=62 * 1024 * 1024),
        cost_estimate=pl.CostEstimate(flops=size * 200, bytes_accessed=size * 4, transcendentals=0),
    )(queries, out_grad, keys, values)


def unpack_split_kernel(parts, *refs):
    buf = refs[-1]
    for k in range(parts):
        buf[jnp.bitwise_xor(lax.axis_index("cp"), k)] = refs[k][...]
    unpack_kernel(buf, *refs[parts:-1])


def unpack_split_call(chunks, prev, unit, piece, shapes):
    parts = len(chunks)
    tokens, wide = chunks[0].shape
    dim = shapes[0].shape[3]
    big, small, _ = unit_specs(unit, parts, dim, piece * tokens // TB)
    size = parts * tokens * wide
    return pl.pallas_call(
        functools.partial(unpack_split_kernel, parts),
        grid=(1, tokens // TB),
        in_specs=[pl.BlockSpec((TB, wide), lambda u, i: (i, 0))] * parts + [pl.BlockSpec(memory_space=pl.ANY)] * len(prev),
        out_specs=[big, big, small, small],
        out_shape=shapes,
        input_output_aliases={i + parts: i for i in range(len(prev))},
        scratch_shapes=[pltpu.VMEM((parts, TB, wide), jnp.bfloat16)],
        compiler_params=pltpu.CompilerParams(dimension_semantics=("arbitrary", "arbitrary"), vmem_limit_bytes=62 * 1024 * 1024),
        cost_estimate=pl.CostEstimate(flops=size * 200, bytes_accessed=size * 4, transcendentals=0),
    )(*chunks, *prev)


def lse_split_kernel(counts, *refs):
    ins, outs = refs[:len(counts)], refs[len(counts):]
    tokens = outs[0].shape[1]
    for k, out in enumerate(outs):
        row = 0
        for ref, count in zip(ins, counts):
            for unit in range(count):
                out[row:row + 2, :] = ref[unit, :, peer_rows(k, tokens)]
                row += 2


def lse_join_kernel(*refs):
    *ins, out = refs
    batch = out.shape[0]
    parts = len(ins)
    for k, ref in enumerate(ins):
        peer = jnp.bitwise_xor(lax.axis_index("cp"), k)
        for row in range(4 * batch):
            group, lane = divmod(row % 4, 2)
            out[row // 4, pl.ds(2 * parts * group + 2 * peer + lane, 1), :] = ref[row:row + 1, :]


def lse_split_call(sums, parts):
    rows = 2 * sum(arr.shape[0] for arr in sums)
    tokens = sums[0].shape[2] // parts
    vmem = pl.BlockSpec(memory_space=pltpu.VMEM)
    return pl.pallas_call(
        functools.partial(lse_split_kernel, [arr.shape[0] for arr in sums]),
        in_specs=[vmem] * len(sums),
        out_specs=[vmem] * parts,
        out_shape=[jax.ShapeDtypeStruct((rows, tokens), jnp.float32)] * parts,
        cost_estimate=pl.CostEstimate(flops=10 ** 7, bytes_accessed=rows * tokens * parts * 8, transcendentals=0),
    )(*sums)


def lse_join_call(chunks, batch):
    rows, tokens = chunks[0].shape
    vmem = pl.BlockSpec(memory_space=pltpu.VMEM)
    return pl.pallas_call(
        lse_join_kernel,
        in_specs=[vmem] * len(chunks),
        out_specs=vmem,
        out_shape=jax.ShapeDtypeStruct((batch, rows * len(chunks) // batch, tokens), jnp.float32),
        cost_estimate=pl.CostEstimate(flops=10 ** 7, bytes_accessed=rows * tokens * len(chunks) * 8, transcendentals=0),
    )(*chunks)


def exchange(chunks):
    size = len(chunks)
    out = [chunks[0]]
    for offset in range(1, size):
        pairs = [(rank, rank ^ offset) for rank in range(size)]
        out.append(lax.ppermute(chunks[offset], "cp", pairs))
    return out


TAIL = 2


def solution(mesh):
    cp_size = mesh.shape["cp"]

    def attention_shard(queries, keys, values, out_grad):
        batch, tokens, _, dim = queries.shape
        units = 2 * batch
        ys, sums = [], []
        for unit in range(units):
            packed = pack_split_call(queries, out_grad, keys, values, unit, cp_size)
            ready = exchange(packed)
            y, lse = attention_split_call(ready, TAIL if unit == units - 1 else 1, cp_size, cp_size * tokens, dim)
            ys.append(y)
            sums.append(lse)
        lse = lse_split_call(sums, cp_size)
        lse = exchange(lse)
        lse = lse_join_call(lse, batch)
        big = jax.ShapeDtypeStruct(queries.shape, jnp.bfloat16)
        small = jax.ShapeDtypeStruct(keys.shape, jnp.bfloat16)
        outs = ()
        for unit, y in enumerate(ys):
            for piece in range(len(y) // cp_size):
                chunks = exchange(y[piece * cp_size:(piece + 1) * cp_size])
                outs = unpack_split_call(chunks, outs, unit, piece, (big, big, small, small))
        return outs[0], lse, outs[1], outs[2], outs[3]

    seq_spec = P("dp", "cp")
    return jax.shard_map(attention_shard, mesh=mesh, in_specs=(seq_spec, seq_spec, seq_spec, seq_spec), out_specs=(seq_spec, P("dp", None, "cp"), seq_spec, seq_spec, seq_spec), check_vma=False)
```

time: 714 us -> 880 us (1.23)
  waiting for transfers between devices: 228 us -> 334 us
  starting transfers between devices: 25.8 us -> 116 us
  Pallas kernels: 455 us -> 420 us
    ppermute x0 -> x98, waiting for transfers between devices: none -> 334 us  [exchange(): out.append(lax.ppermute(chunks[offset], 'cp', pairs))]
    all_to_all x7 -> x0, waiting for transfers between devices: 228 us -> none  [the longest x3 130 us: attention_shard(): ready.append(lax.all_to_all(packed, 'cp', 0, 0, tiled=True))]
    ppermute x0 -> x98, starting transfers between devices: none -> 116 us  [exchange(): out.append(lax.ppermute(chunks[offset], 'cp', pairs))]
    pallas_call x10 -> x21, Pallas kernels: 455 us -> 420 us  [the longest x6 334 us: attention_split_call(): pl.pallas_call(functools.partial(attention_split_kernel, split_in, split_...]
    all_to_all x7 -> x0, starting transfers between devices: 25.8 us -> none  [the longest x3 12.3 us: attention_shard(): ready.append(lax.all_to_all(packed, 'cp', 0, 0, tiled=True))]
  transfers between devices with their start and end apart: 7 -> 98, of which waited for: 6 -> 30; matrix products, arithmetic and copies ran while one was open for 0% -> 0% of each run, Pallas kernels for 62% -> 47%
where the time goes in v3:
time: 880 us; the launch traced here: 877 us
  Pallas kernels  420 us (48%)
  waiting for transfers between devices  334 us (38%)
  starting transfers between devices  116 us (13%)
    ppermute x98, waiting for transfers between devices, exchange(): out.append(lax.ppermute(chunks[offset], 'cp', pairs))  334 us
    pallas_call x6, Pallas kernels, attention_split_call(): pl.pallas_call(functools.partial(attention_split_kernel, split_in, split_...  334 us
    ppermute x98, starting transfers between devices, exchange(): out.append(lax.ppermute(chunks[offset], 'cp', pairs))  116 us
    pallas_call x7, Pallas kernels, unpack_split_call(): pl.pallas_call(functools.partial(unpack_split_kernel, parts), grid=(1, to...  44.3 us
    pallas_call x6, Pallas kernels, pack_split_call(): pl.pallas_call(pack_split_kernel, grid=(1, tokens // TB), in_specs=[big,...  39 us
  transfers between devices with their start and end apart: 98, of which 30 were waited for; matrix products, arithmetic and copies ran while one was open for 0% of the time, Pallas kernels for 47%

profile of v3, /device:TPU:0, one launch (start us, length us, event | category | flops | bytes accessed | tf_op | source)
XLA Modules:
  0.0 877.1 jit_solution(13124989342912671728)
XLA Ops:
  14.9 10.0 %collective-permute-done.50.refs_2_ = bf16[384,768]{1,0:T(8,128)(2,1)} collective-permute-done((bf16[384,768]{1,0:T(8,128)(2,1)}, bf16[384,768]{1,0:T(8,128)(2,1)}, u32[]{:S(2)}, u32[]{:S(2)}) %collective-permute-start.50) | collective-permute-done | bytes 589856 | tf_op jit(solution)/shard_map/ppermute | solution.py:347
  39.8 23.9 %collective-permute-done.53.refs_5_ = bf16[384,768]{1,0:T(8,128)(2,1)} collective-permute-done((bf16[384,768]{1,0:T(8,128)(2,1)}, bf16[384,768]{1,0:T(8,128)(2,1)}, u32[]{:S(2)}, u32[]{:S(2)}) %collective-permute-start.53) | collective-permute-done | bytes 589856 | tf_op jit(solution)/shard_map/ppermute | solution.py:347
  77.3 10.5 %collective-permute-done.37.refs_3_ = bf16[384,768]{1,0:T(8,128)(2,1)S(1)} collective-permute-done((bf16[384,768]{1,0:T(8,128)(2,1)}, bf16[384,768]{1,0:T(8,128)(2,1)S(1)}, u32[]{:S(2)}, u32[]{:S(2)}) %collective-permute-start.37) | collective-permute-done | bytes 589856 | tf_op jit(solution)/shard_map/ppermute | solution.py:347
  91.1 26.9 %collective-permute-done.39.refs_5_ = bf16[384,768]{1,0:T(8,128)(2,1)} collective-permute-done((bf16[384,768]{1,0:T(8,128)(2,1)}, bf16[384,768]{1,0:T(8,128)(2,1)}, u32[]{:S(2)}, u32[]{:S(2)}) %collective-permute-start.39) | collective-permute-done | bytes 589856 | tf_op jit(solution)/shard_map/ppermute | solution.py:347
  143.5 55.5 %shard_map.90 = (bf16[384,768]{1,0:T(8,128)(2,1)}, bf16[384,768]{1,0:T(8,128)(2,1)}, bf16[384,768]{1,0:T(8,128)(2,1)}, bf16[384,768]{1,0:T(8,128)(2,1)}, bf16[38...) custom-call(bf16[384,768]{1,0:T(8,128)(2,1)} %get-tuple-element.207., ...), custom_call_target="tpu_custom_call" | custom-call | flops 14495514624 | bytes 9437184 | tf_op jit(solution)/shard_map/pallas_call | solution.py:229
  204.9 55.7 %shard_map.88 = (bf16[384,768]{1,0:T(8,128)(2,1)}, bf16[384,768]{1,0:T(8,128)(2,1)}, bf16[384,768]{1,0:T(8,128)(2,1)}, bf16[384,768]{1,0:T(8,128)(2,1)}, bf16[38...) custom-call(bf16[384,768]{1,0:T(8,128)(2,1)} %get-tuple-element.191., ...), custom_call_target="tpu_custom_call" | custom-call | flops 14495514624 | bytes 9437184 | tf_op jit(solution)/shard_map/pallas_call | solution.py:229
  264.4 55.7 %shard_map.86 = (bf16[384,768]{1,0:T(8,128)(2,1)}, bf16[384,768]{1,0:T(8,128)(2,1)}, bf16[384,768]{1,0:T(8,128)(2,1)}, bf16[384,768]{1,0:T(8,128)(2,1)}, bf16[38...) custom-call(bf16[384,768]{1,0:T(8,128)(2,1)} %get-tuple-element.175., ...), custom_call_target="tpu_custom_call" | custom-call | flops 14495514624 | bytes 9437184 | tf_op jit(solution)/shard_map/pallas_call | solution.py:229
  325.3 55.6 %shard_map.84 = (bf16[192,768]{1,0:T(8,128)(2,1)}, bf16[192,768]{1,0:T(8,128)(2,1)}, bf16[192,768]{1,0:T(8,128)(2,1)}, bf16[192,768]{1,0:T(8,128)(2,1)}, bf16[19...) custom-call(bf16[384,768]{1,0:T(8,128)(2,1)} %get-tuple-element.151., ...), custom_call_target="tpu_custom_call" | custom-call | flops 14495514624 | bytes 9437184 | tf_op jit(solution)/shard_map/pallas_call | solution.py:229
  385.6 55.8 %shard_map.94 = (bf16[384,768]{1,0:T(8,128)(2,1)}, bf16[384,768]{1,0:T(8,128)(2,1)}, bf16[384,768]{1,0:T(8,128)(2,1)}, bf16[384,768]{1,0:T(8,128)(2,1)}, bf16[38...) custom-call(bf16[384,768]{1,0:T(8,128)(2,1)} %get-tuple-element.239., ...), custom_call_target="tpu_custom_call" | custom-call | flops 14495514624 | bytes 9437184 | tf_op jit(solution)/shard_map/pallas_call | solution.py:229
  444.0 55.6 %shard_map.92 = (bf16[384,768]{1,0:T(8,128)(2,1)}, bf16[384,768]{1,0:T(8,128)(2,1)}, bf16[384,768]{1,0:T(8,128)(2,1)}, bf16[384,768]{1,0:T(8,128)(2,1)}, bf16[38...) custom-call(bf16[384,768]{1,0:T(8,128)(2,1)} %get-tuple-element.223., ...), custom_call_target="tpu_custom_call" | custom-call | flops 14495514624 | bytes 9437184 | tf_op jit(solution)/shard_map/pallas_call | solution.py:229
  538.7 13.7 %collective-permute-start.57 = (bf16[384,768]{1,0:T(8,128)(2,1)}, bf16[384,768]{1,0:T(8,128)(2,1)S(1)}, u32[]{:S(2)}, u32[]{:S(2)}) collective-permute-start(bf16[384,768]{1,0:T(8,128)(2,1)} %get-tuple-element.217), channel_id=1, source_target_pairs={{0,2},{1,3},{2,0},{3,1},{4,6},{5,7},{6,4},{7,5}} | collective-permute-start | bytes 1769480 | tf_op jit(solution)/shard_map/ppermute | solution.py:347
  567.3 12.2 %collective-permute-done.58.refs_3_ = bf16[384,768]{1,0:T(8,128)(2,1)S(1)} collective-permute-done((bf16[384,768]{1,0:T(8,128)(2,1)}, bf16[384,768]{1,0:T(8,128)(2,1)S(1)}, u32[]{:S(2)}, u32[]{:S(2)}) %collective-permute-start.58) | collective-permute-done | bytes 589856 | tf_op jit(solution)/shard_map/ppermute | solution.py:347
  581.6 30.6 %collective-permute-done.60.refs_5_ = bf16[384,768]{1,0:T(8,128)(2,1)S(1)} collective-permute-done((bf16[384,768]{1,0:T(8,128)(2,1)}, bf16[384,768]{1,0:T(8,128)(2,1)S(1)}, u32[]{:S(2)}, u32[]{:S(2)}) %collective-permute-start.60) | collective-permute-done | bytes 589856 | tf_op jit(solution)/shard_map/ppermute | solution.py:347
  617.9 12.1 %collective-permute-done.44.refs_3_ = bf16[384,768]{1,0:T(8,128)(2,1)S(1)} collective-permute-done((bf16[384,768]{1,0:T(8,128)(2,1)}, bf16[384,768]{1,0:T(8,128)(2,1)S(1)}, u32[]{:S(2)}, u32[]{:S(2)}) %collective-permute-start.44) | collective-permute-done | bytes 589856 | tf_op jit(solution)/shard_map/ppermute | solution.py:347
  632.2 34.0 %collective-permute-done.46.refs_5_ = bf16[384,768]{1,0:T(8,128)(2,1)S(1)} collective-permute-done((bf16[384,768]{1,0:T(8,128)(2,1)}, bf16[384,768]{1,0:T(8,128)(2,1)S(1)}, u32[]{:S(2)}, u32[]{:S(2)}) %collective-permute-start.46) | collective-permute-done | bytes 589856 | tf_op jit(solution)/shard_map/ppermute | solution.py:347
  671.9 9.6 %collective-permute-done.30.refs_3_ = bf16[384,768]{1,0:T(8,128)(2,1)S(1)} collective-permute-done((bf16[384,768]{1,0:T(8,128)(2,1)}, bf16[384,768]{1,0:T(8,128)(2,1)S(1)}, u32[]{:S(2)}, u32[]{:S(2)}) %collective-permute-start.30) | collective-permute-done | bytes 589856 | tf_op jit(solution)/shard_map/ppermute | solution.py:347
  683.3 25.8 %collective-permute-done.31.refs_4_ = bf16[384,768]{1,0:T(8,128)(2,1)S(1)} collective-permute-done((bf16[384,768]{1,0:T(8,128)(2,1)}, bf16[384,768]{1,0:T(8,128)(2,1)S(1)}, u32[]{:S(2)}, u32[]{:S(2)}) %collective-permute-start.31) | collective-permute-done | bytes 589856 | tf_op jit(solution)/shard_map/ppermute | solution.py:347
  710.5 8.9 %collective-permute-done.32.refs_5_ = bf16[384,768]{1,0:T(8,128)(2,1)S(1)} collective-permute-done((bf16[384,768]{1,0:T(8,128)(2,1)}, bf16[384,768]{1,0:T(8,128)(2,1)S(1)}, u32[]{:S(2)}, u32[]{:S(2)}) %collective-permute-start.32) | collective-permute-done | bytes 589856 | tf_op jit(solution)/shard_map/ppermute | solution.py:347
  725.6 9.6 %collective-permute-done.86.refs_3_ = bf16[384,768]{1,0:T(8,128)(2,1)S(1)} collective-permute-done((bf16[384,768]{1,0:T(8,128)(2,1)}, bf16[384,768]{1,0:T(8,128)(2,1)S(1)}, u32[]{:S(2)}, u32[]{:S(2)}) %collective-permute-start.86) | collective-permute-done | bytes 589856 | tf_op jit(solution)/shard_map/ppermute | solution.py:347
  736.6 26.3 %collective-permute-done.87.refs_4_ = bf16[384,768]{1,0:T(8,128)(2,1)} collective-permute-done((bf16[384,768]{1,0:T(8,128)(2,1)}, bf16[384,768]{1,0:T(8,128)(2,1)}, u32[]{:S(2)}, u32[]{:S(2)}) %collective-permute-start.87) | collective-permute-done | bytes 589856 | tf_op jit(solution)/shard_map/ppermute | solution.py:347
  763.8 8.8 %collective-permute-done.88.refs_5_ = bf16[384,768]{1,0:T(8,128)(2,1)} collective-permute-done((bf16[384,768]{1,0:T(8,128)(2,1)}, bf16[384,768]{1,0:T(8,128)(2,1)}, u32[]{:S(2)}, u32[]{:S(2)}) %collective-permute-start.88) | collective-permute-done | bytes 589856 | tf_op jit(solution)/shard_map/ppermute | solution.py:347
  779.1 9.5 %collective-permute-done.72.refs_3_ = bf16[384,768]{1,0:T(8,128)(2,1)S(1)} collective-permute-done((bf16[384,768]{1,0:T(8,128)(2,1)}, bf16[384,768]{1,0:T(8,128)(2,1)S(1)}, u32[]{:S(2)}, u32[]{:S(2)}) %collective-permute-start.72) | collective-permute-done | bytes 589856 | tf_op jit(solution)/shard_map/ppermute | solution.py:347
  790.7 25.5 %collective-permute-done.73.refs_4_ = bf16[384,768]{1,0:T(8,128)(2,1)S(1)} collective-permute-done((bf16[384,768]{1,0:T(8,128)(2,1)}, bf16[384,768]{1,0:T(8,128)(2,1)S(1)}, u32[]{:S(2)}, u32[]{:S(2)}) %collective-permute-start.73) | collective-permute-done | bytes 589856 | tf_op jit(solution)/shard_map/ppermute | solution.py:347
  818.2 9.4 %collective-permute-done.74.refs_5_ = bf16[384,768]{1,0:T(8,128)(2,1)} collective-permute-done((bf16[384,768]{1,0:T(8,128)(2,1)}, bf16[384,768]{1,0:T(8,128)(2,1)}, u32[]{:S(2)}, u32[]{:S(2)}) %collective-permute-start.74) | collective-permute-done | bytes 589856 | tf_op jit(solution)/shard_map/ppermute | solution.py:347
  (301 shorter events, 234.5 us)
Async XLA Ops:
  73.8 65.1 %collective-permute-start.40 = (bf16[384,768]{1,0:T(8,128)(2,1)}, bf16[384,768]{1,0:T(8,128)(2,1)}, u32[]{:S(2)}, u32[]{:S(2)}) collective-permute-start(bf16[384,768]{1,0:T(8,128)(2,1)} %get-tuple-element.197), channel_id=1, source_target_pairs={{0,6},{1,7},{2,4},{3,5},{4,2},{5,3},{6,0},{7,1}} | collective-permute-start | bytes 1769480 | tf_op jit(solution)/shard_map/ppermute | solution.py:347
  75.5 65.0 %collective-permute-start.41 = (bf16[384,768]{1,0:T(8,128)(2,1)}, bf16[384,768]{1,0:T(8,128)(2,1)}, u32[]{:S(2)}, u32[]{:S(2)}) collective-permute-start(bf16[384,768]{1,0:T(8,128)(2,1)} %get-tuple-element.198), channel_id=1, source_target_pairs={{0,7},{1,6},{2,5},{3,4},{4,3},{5,2},{6,1},{7,0}} | collective-permute-start | bytes 1769480 | tf_op jit(solution)/shard_map/ppermute | solution.py:347
  140.5 60.3 %collective-permute-start.26 = (bf16[384,768]{1,0:T(8,128)(2,1)}, bf16[384,768]{1,0:T(8,128)(2,1)}, u32[]{:S(2)}, u32[]{:S(2)}) collective-permute-start(bf16[384,768]{1,0:T(8,128)(2,1)} %get-tuple-element.181), channel_id=1, source_target_pairs={{0,6},{1,7},{2,4},{3,5},{4,2},{5,3},{6,0},{7,1}} | collective-permute-start | bytes 1769480 | tf_op jit(solution)/shard_map/ppermute | solution.py:347
  142.0 60.4 %collective-permute-start.27 = (bf16[384,768]{1,0:T(8,128)(2,1)}, bf16[384,768]{1,0:T(8,128)(2,1)}, u32[]{:S(2)}, u32[]{:S(2)}) collective-permute-start(bf16[384,768]{1,0:T(8,128)(2,1)} %get-tuple-element.182), channel_id=1, source_target_pairs={{0,7},{1,6},{2,5},{3,4},{4,3},{5,2},{6,1},{7,0}} | collective-permute-start | bytes 1769480 | tf_op jit(solution)/shard_map/ppermute | solution.py:347
  199.1 61.5 %collective-permute-start.1 = (bf16[384,768]{1,0:T(8,128)(2,1)}, bf16[384,768]{1,0:T(8,128)(2,1)}, u32[]{:S(2)}, u32[]{:S(2)}) collective-permute-start(bf16[384,768]{1,0:T(8,128)(2,1)} %get-tuple-element.153), channel_id=1, source_target_pairs={{0,2},{1,3},{2,0},{3,1},{4,6},{5,7},{6,4},{7,5}} | collective-permute-start | bytes 1769480 | tf_op jit(solution)/shard_map/ppermute | solution.py:347
  200.6 61.0 %collective-permute-start.2 = (bf16[384,768]{1,0:T(8,128)(2,1)}, bf16[384,768]{1,0:T(8,128)(2,1)}, u32[]{:S(2)}, u32[]{:S(2)}) collective-permute-start(bf16[384,768]{1,0:T(8,128)(2,1)} %get-tuple-element.154), channel_id=1, source_target_pairs={{0,3},{1,2},{2,1},{3,0},{4,7},{5,6},{6,5},{7,4}} | collective-permute-start | bytes 1769480 | tf_op jit(solution)/shard_map/ppermute | solution.py:347
  200.8 60.8 %collective-permute-start.3 = (bf16[384,768]{1,0:T(8,128)(2,1)}, bf16[384,768]{1,0:T(8,128)(2,1)}, u32[]{:S(2)}, u32[]{:S(2)}) collective-permute-start(bf16[384,768]{1,0:T(8,128)(2,1)} %get-tuple-element.155), channel_id=1, source_target_pairs={{0,4},{1,5},{2,6},{3,7},{4,0},{5,1},{6,2},{7,3}} | collective-permute-start | bytes 1769480 | tf_op jit(solution)/shard_map/ppermute | solution.py:347
  202.3 60.6 %collective-permute-start.4 = (bf16[384,768]{1,0:T(8,128)(2,1)}, bf16[384,768]{1,0:T(8,128)(2,1)}, u32[]{:S(2)}, u32[]{:S(2)}) collective-permute-start(bf16[384,768]{1,0:T(8,128)(2,1)} %get-tuple-element.156), channel_id=1, source_target_pairs={{0,5},{1,4},{2,7},{3,6},{4,1},{5,0},{6,3},{7,2}} | collective-permute-start | bytes 1769480 | tf_op jit(solution)/shard_map/ppermute | solution.py:347
  202.6 60.8 %collective-permute-start.5 = (bf16[384,768]{1,0:T(8,128)(2,1)}, bf16[384,768]{1,0:T(8,128)(2,1)}, u32[]{:S(2)}, u32[]{:S(2)}) collective-permute-start(bf16[384,768]{1,0:T(8,128)(2,1)} %get-tuple-element.157), channel_id=1, source_target_pairs={{0,6},{1,7},{2,4},{3,5},{4,2},{5,3},{6,0},{7,1}} | collective-permute-start | bytes 1769480 | tf_op jit(solution)/shard_map/ppermute | solution.py:347
  261.6 61.4 %collective-permute-start.78 = (bf16[384,768]{1,0:T(8,128)(2,1)S(1)}, bf16[384,768]{1,0:T(8,128)(2,1)}, u32[]{:S(2)}, u32[]{:S(2)}) collective-permute-start(bf16[384,768]{1,0:T(8,128)(2,1)S(1)} %copy-done.48), channel_id=1, source_target_pairs={{0,2},{1,3},{2,0},{3,1},{4,6},{5,7},{6,4},{7,5}} | collective-permute-start | bytes 1769480 | tf_op jit(solution)/shard_map/ppermute | solution.py:347
  263.0 60.7 %collective-permute-start.79 = (bf16[384,768]{1,0:T(8,128)(2,1)S(1)}, bf16[384,768]{1,0:T(8,128)(2,1)}, u32[]{:S(2)}, u32[]{:S(2)}) collective-permute-start(bf16[384,768]{1,0:T(8,128)(2,1)S(1)} %copy-done.45), channel_id=1, source_target_pairs={{0,3},{1,2},{2,1},{3,0},{4,7},{5,6},{6,5},{7,4}} | collective-permute-start | bytes 1769480 | tf_op jit(solution)/shard_map/ppermute | solution.py:347
  263.4 60.5 %collective-permute-start.80 = (bf16[384,768]{1,0:T(8,128)(2,1)S(1)}, bf16[384,768]{1,0:T(8,128)(2,1)}, u32[]{:S(2)}, u32[]{:S(2)}) collective-permute-start(bf16[384,768]{1,0:T(8,128)(2,1)S(1)} %copy-done.43), channel_id=1, source_target_pairs={{0,4},{1,5},{2,6},{3,7},{4,0},{5,1},{6,2},{7,3}} | collective-permute-start | bytes 1769480 | tf_op jit(solution)/shard_map/ppermute | solution.py:347
  320.2 60.8 %collective-permute-start.81 = (bf16[384,768]{1,0:T(8,128)(2,1)}, bf16[384,768]{1,0:T(8,128)(2,1)}, u32[]{:S(2)}, u32[]{:S(2)}) collective-permute-start(bf16[384,768]{1,0:T(8,128)(2,1)} %get-tuple-element.244), channel_id=1, source_target_pairs={{0,5},{1,4},{2,7},{3,6},{4,1},{5,0},{6,3},{7,2}} | collective-permute-start | bytes 1769480 | tf_op jit(solution)/shard_map/ppermute | solution.py:347
  320.9 60.3 %collective-permute-start.82 = (bf16[384,768]{1,0:T(8,128)(2,1)}, bf16[384,768]{1,0:T(8,128)(2,1)}, u32[]{:S(2)}, u32[]{:S(2)}) collective-permute-start(bf16[384,768]{1,0:T(8,128)(2,1)} %get-tuple-element.245), channel_id=1, source_target_pairs={{0,6},{1,7},{2,4},{3,5},{4,2},{5,3},{6,0},{7,1}} | collective-permute-start | bytes 1769480 | tf_op jit(solution)/shard_map/ppermute | solution.py:347
  323.9 61.3 %collective-permute-start.64 = (bf16[384,768]{1,0:T(8,128)(2,1)}, bf16[384,768]{1,0:T(8,128)(2,1)}, u32[]{:S(2)}, u32[]{:S(2)}) collective-permute-start(bf16[384,768]{1,0:T(8,128)(2,1)} %get-tuple-element.225), channel_id=1, source_target_pairs={{0,2},{1,3},{2,0},{3,1},{4,6},{5,7},{6,4},{7,5}} | collective-permute-start | bytes 1769480 | tf_op jit(solution)/shard_map/ppermute | solution.py:347
  381.0 60.4 %collective-permute-start.65 = (bf16[384,768]{1,0:T(8,128)(2,1)S(1)}, bf16[384,768]{1,0:T(8,128)(2,1)}, u32[]{:S(2)}, u32[]{:S(2)}) collective-permute-start(bf16[384,768]{1,0:T(8,128)(2,1)S(1)} %copy-done.42), channel_id=1, source_target_pairs={{0,3},{1,2},{2,1},{3,0},{4,7},{5,6},{6,5},{7,4}} | collective-permute-start | bytes 1769480 | tf_op jit(solution)/shard_map/ppermute | solution.py:347
  381.2 60.8 %collective-permute-start.66 = (bf16[384,768]{1,0:T(8,128)(2,1)}, bf16[384,768]{1,0:T(8,128)(2,1)}, u32[]{:S(2)}, u32[]{:S(2)}) collective-permute-start(bf16[384,768]{1,0:T(8,128)(2,1)} %get-tuple-element.227), channel_id=1, source_target_pairs={{0,4},{1,5},{2,6},{3,7},{4,0},{5,1},{6,2},{7,3}} | collective-permute-start | bytes 1769480 | tf_op jit(solution)/shard_map/ppermute | solution.py:347
  382.4 61.0 %collective-permute-start.67 = (bf16[384,768]{1,0:T(8,128)(2,1)S(1)}, bf16[384,768]{1,0:T(8,128)(2,1)}, u32[]{:S(2)}, u32[]{:S(2)}) collective-permute-start(bf16[384,768]{1,0:T(8,128)(2,1)S(1)} %copy-done.41), channel_id=1, source_target_pairs={{0,5},{1,4},{2,7},{3,6},{4,1},{5,0},{6,3},{7,2}} | collective-permute-start | bytes 1769480 | tf_op jit(solution)/shard_map/ppermute | solution.py:347
  383.1 60.2 %collective-permute-start.68 = (bf16[384,768]{1,0:T(8,128)(2,1)}, bf16[384,768]{1,0:T(8,128)(2,1)}, u32[]{:S(2)}, u32[]{:S(2)}) collective-permute-start(bf16[384,768]{1,0:T(8,128)(2,1)} %get-tuple-element.229), channel_id=1, source_target_pairs={{0,6},{1,7},{2,4},{3,5},{4,2},{5,3},{6,0},{7,1}} | collective-permute-start | bytes 1769480 | tf_op jit(solution)/shard_map/ppermute | solution.py:347
  441.3 86.4 %collective-permute-start.7 = (bf16[192,768]{1,0:T(8,128)(2,1)}, bf16[192,768]{1,0:T(8,128)(2,1)S(1)}, u32[]{:S(2)}, u32[]{:S(2)}) collective-permute-start(bf16[192,768]{1,0:T(8,128)(2,1)} %get-tuple-element.160), channel_id=1, source_target_pairs={{0,1},{1,0},{2,3},{3,2},{4,5},{5,4},{6,7},{7,6}} | collective-permute-start | bytes 884744 | tf_op jit(solution)/shard_map/ppermute | solution.py:347
  442.0 87.0 %collective-permute-start.8 = (bf16[192,768]{1,0:T(8,128)(2,1)}, bf16[192,768]{1,0:T(8,128)(2,1)S(1)}, u32[]{:S(2)}, u32[]{:S(2)}) collective-permute-start(bf16[192,768]{1,0:T(8,128)(2,1)} %get-tuple-element.161), channel_id=1, source_target_pairs={{0,2},{1,3},{2,0},{3,1},{4,6},{5,7},{6,4},{7,5}} | collective-permute-start | bytes 884744 | tf_op jit(solution)/shard_map/ppermute | solution.py:347
  443.3 87.1 %collective-permute-start.14 = (bf16[192,768]{1,0:T(8,128)(2,1)}, bf16[192,768]{1,0:T(8,128)(2,1)S(1)}, u32[]{:S(2)}, u32[]{:S(2)}) collective-permute-start(bf16[192,768]{1,0:T(8,128)(2,1)} %get-tuple-element.168), channel_id=1, source_target_pairs={{0,1},{1,0},{2,3},{3,2},{4,5},{5,4},{6,7},{7,6}} | collective-permute-start | bytes 884744 | tf_op jit(solution)/shard_map/ppermute | solution.py:347
  443.3 88.6 %collective-permute-start.15 = (bf16[192,768]{1,0:T(8,128)(2,1)}, bf16[192,768]{1,0:T(8,128)(2,1)S(1)}, u32[]{:S(2)}, u32[]{:S(2)}) collective-permute-start(bf16[192,768]{1,0:T(8,128)(2,1)} %get-tuple-element.169), channel_id=1, source_target_pairs={{0,2},{1,3},{2,0},{3,1},{4,6},{5,7},{6,4},{7,5}} | collective-permute-start | bytes 884744 | tf_op jit(solution)/shard_map/ppermute | solution.py:347
  788.5 83.9 %collective-permute-start.9 = (bf16[192,768]{1,0:T(8,128)(2,1)}, bf16[192,768]{1,0:T(8,128)(2,1)}, u32[]{:S(2)}, u32[]{:S(2)}) collective-permute-start(bf16[192,768]{1,0:T(8,128)(2,1)} %get-tuple-element.162), channel_id=1, source_target_pairs={{0,3},{1,2},{2,1},{3,0},{4,7},{5,6},{6,5},{7,4}} | collective-permute-start | bytes 884744 | tf_op jit(solution)/shard_map/ppermute | solution.py:347
  (128 other events, 7597.3 us)

commit v4 on v3

--- a/solution.py
+++ b/solution.py
@@ -196,15 +196,15 @@
 
 
 def attention_split_kernel(split_in, split_out, parts, *refs):
-    count_in, count_out = (parts if split_in else 1), parts * split_out
+    count_in, count_out = parts * split_in, parts * split_out
     ins, outs, lse_ref = refs[:count_in], refs[count_in:count_in + count_out], refs[count_in + count_out]
     scratch = refs[count_in + count_out + 1:]
     x_ref, y_ref, sems = scratch[-3:]
     tokens = x_ref.shape[0] // parts
-    if split_in:
-        copies = [pltpu.make_async_copy(ref, x_ref.at[peer_rows(k, tokens)], sems.at[k]) for k, ref in enumerate(ins)]
-    else:
-        copies = [pltpu.make_async_copy(ins[0], x_ref, sems.at[0])]
+    copies = [
+        pltpu.make_async_copy(ref, x_ref.at[peer_rows(idx % parts, tokens, idx // parts, split_in)], sems.at[idx])
+        for idx, ref in enumerate(ins)
+    ]
     for copy in copies:
         copy.start()
     for copy in copies:
@@ -222,7 +222,7 @@
 
 def attention_split_call(ins, split_out, parts, seq, dim):
     wide = 6 * dim
-    split_in = len(ins) > 1
+    split_in = len(ins) // parts
     pairs = seq * seq
     any_spec = pl.BlockSpec(memory_space=pl.ANY)
     y_shapes = [jax.ShapeDtypeStruct((seq // parts // split_out, wide), jnp.bfloat16)] * (parts * split_out)
@@ -234,7 +234,7 @@
         scratch_shapes=attention_scratch(seq, dim) + [
             pltpu.VMEM((seq, wide), jnp.bfloat16),
             pltpu.VMEM((seq, wide), jnp.bfloat16),
-            pltpu.SemaphoreType.DMA((2 * parts,)),
+            pltpu.SemaphoreType.DMA((3 * parts,)),
         ],
         compiler_params=pltpu.CompilerParams(vmem_limit_bytes=62 * 1024 * 1024),
         cost_estimate=pl.CostEstimate(flops=pairs * dim * 12, bytes_accessed=seq * wide * 4, transcendentals=pairs * 2),
@@ -249,9 +249,9 @@
         ref[...] = buf[jnp.bitwise_xor(lax.axis_index("cp"), k)]
 
 
-def pack_split_call(queries, out_grad, keys, values, unit, parts):
-    tokens, dim = queries.shape[1], queries.shape[3]
-    big, small, _ = unit_specs(unit, parts, dim)
+def pack_split_call(queries, out_grad, keys, values, unit, piece, pieces, parts):
+    tokens, dim = queries.shape[1] // pieces, queries.shape[3]
+    big, small, _ = unit_specs(unit, parts, dim, piece * tokens // TB)
     wide = 6 * dim
     size = parts * tokens * wide
     return pl.pallas_call(
@@ -348,7 +348,8 @@
     return out
 
 
-TAIL = 2
+HEAD = 2
+TAIL = 3
 
 
 def solution(mesh):
@@ -359,8 +360,11 @@
         units = 2 * batch
         ys, sums = [], []
         for unit in range(units):
-            packed = pack_split_call(queries, out_grad, keys, values, unit, cp_size)
-            ready = exchange(packed)
+            ready = []
+            pieces = HEAD if unit == 0 else 1
+            for piece in range(pieces):
+                packed = pack_split_call(queries, out_grad, keys, values, unit, piece, pieces, cp_size)
+                ready += exchange(packed)
             y, lse = attention_split_call(ready, TAIL if unit == units - 1 else 1, cp_size, cp_size * tokens, dim)
             ys.append(y)
             sums.append(lse)

time: 880 us -> 843 us (0.958)
  waiting for transfers between devices: 334 us -> 301 us
    ppermute x98 -> x112, waiting for transfers between devices: 334 us -> 301 us  [exchange(): out.append(lax.ppermute(chunks[offset], 'cp', pairs))]
    ppermute x98 -> x112, starting transfers between devices: 116 us -> 113 us  [exchange(): out.append(lax.ppermute(chunks[offset], 'cp', pairs))]
    pallas_call x6 -> x7, Pallas kernels: 39 us -> 40.9 us  [pack_split_call(): pl.pallas_call(pack_split_kernel, grid=(1, tokens // TB), in_specs=[big,...]
    pallas_call x7 -> x8, Pallas kernels: 44.3 us -> 43.6 us  [unpack_split_call(): pl.pallas_call(functools.partial(unpack_split_kernel, parts), grid=(1, to...]
  transfers between devices with their start and end apart: 98 -> 112, of which waited for: 30 -> 40; matrix products, arithmetic and copies ran while one was open for 0% -> 0% of each run, Pallas kernels for 47% -> 49%
where the time goes in v4:
time: 843 us; the launch traced here: 841 us
  Pallas kernels  423 us (50%)
  waiting for transfers between devices  301 us (36%)
  starting transfers between devices  113 us (13%)
    pallas_call x6, Pallas kernels, attention_split_call(): pl.pallas_call(functools.partial(attention_split_kernel, split_in, split_...  335 us
    ppermute x112, waiting for transfers between devices, exchange(): out.append(lax.ppermute(chunks[offset], 'cp', pairs))  301 us
    ppermute x112, starting transfers between devices, exchange(): out.append(lax.ppermute(chunks[offset], 'cp', pairs))  113 us
    pallas_call x8, Pallas kernels, unpack_split_call(): pl.pallas_call(functools.partial(unpack_split_kernel, parts), grid=(1, to...  43.6 us
    pallas_call x7, Pallas kernels, pack_split_call(): pl.pallas_call(pack_split_kernel, grid=(1, tokens // TB), in_specs=[big,...  40.9 us
  transfers between devices with their start and end apart: 112, of which 40 were waited for; matrix products, arithmetic and copies ran while one was open for 0% of the time, Pallas kernels for 49%

profile of v4, /device:TPU:0, one launch (start us, length us, event | category | flops | bytes accessed | tf_op | source)
XLA Modules:
  0.0 841.3 jit_solution(16937186599486730422)
XLA Ops:
  24.7 11.3 %collective-permute-done.95.refs_13_ = bf16[192,768]{1,0:T(8,128)(2,1)S(1)} collective-permute-done((bf16[192,768]{1,0:T(8,128)(2,1)}, bf16[192,768]{1,0:T(8,128)(2,1)S(1)}, u32[]{:S(2)}, u32[]{:S(2)}) %collective-permute-start.95) | collective-permute-done | bytes 294944 | tf_op jit(solution)/shard_map/ppermute | solution.py:347
  90.1 28.5 %collective-permute-done.74.refs_5_ = bf16[384,768]{1,0:T(8,128)(2,1)} collective-permute-done((bf16[384,768]{1,0:T(8,128)(2,1)}, bf16[384,768]{1,0:T(8,128)(2,1)}, u32[]{:S(2)}, u32[]{:S(2)}) %collective-permute-start.74) | collective-permute-done | bytes 589856 | tf_op jit(solution)/shard_map/ppermute | solution.py:347
  144.5 55.6 %shard_map.95 = (bf16[384,768]{1,0:T(8,128)(2,1)}, bf16[384,768]{1,0:T(8,128)(2,1)}, bf16[384,768]{1,0:T(8,128)(2,1)}, bf16[384,768]{1,0:T(8,128)(2,1)}, bf16[38...) custom-call(bf16[192,768]{1,0:T(8,128)(2,1)} %get-tuple-element.267., ...), custom_call_target="tpu_custom_call" | custom-call | flops 14495514624 | bytes 9437184 | tf_op jit(solution)/shard_map/pallas_call | solution.py:229
  205.5 55.9 %shard_map.92 = (bf16[384,768]{1,0:T(8,128)(2,1)}, bf16[384,768]{1,0:T(8,128)(2,1)}, bf16[384,768]{1,0:T(8,128)(2,1)}, bf16[384,768]{1,0:T(8,128)(2,1)}, bf16[38...) custom-call(bf16[384,768]{1,0:T(8,128)(2,1)} %get-tuple-element.251., ...), custom_call_target="tpu_custom_call" | custom-call | flops 14495514624 | bytes 9437184 | tf_op jit(solution)/shard_map/pallas_call | solution.py:229
  264.8 55.5 %shard_map.90 = (bf16[384,768]{1,0:T(8,128)(2,1)}, bf16[384,768]{1,0:T(8,128)(2,1)}, bf16[384,768]{1,0:T(8,128)(2,1)}, bf16[384,768]{1,0:T(8,128)(2,1)}, bf16[38...) custom-call(bf16[384,768]{1,0:T(8,128)(2,1)} %get-tuple-element.235., ...), custom_call_target="tpu_custom_call" | custom-call | flops 14495514624 | bytes 9437184 | tf_op jit(solution)/shard_map/pallas_call | solution.py:229
  325.7 56.0 %shard_map.88 = (bf16[384,768]{1,0:T(8,128)(2,1)}, bf16[384,768]{1,0:T(8,128)(2,1)}, bf16[384,768]{1,0:T(8,128)(2,1)}, bf16[384,768]{1,0:T(8,128)(2,1)}, bf16[38...) custom-call(bf16[384,768]{1,0:T(8,128)(2,1)} %get-tuple-element.219., ...), custom_call_target="tpu_custom_call" | custom-call | flops 14495514624 | bytes 9437184 | tf_op jit(solution)/shard_map/pallas_call | solution.py:229
  387.0 55.6 %shard_map.84 = (bf16[128,768]{1,0:T(8,128)(2,1)}, bf16[128,768]{1,0:T(8,128)(2,1)}, bf16[128,768]{1,0:T(8,128)(2,1)}, bf16[128,768]{1,0:T(8,128)(2,1)}, bf16[12...) custom-call(bf16[384,768]{1,0:T(8,128)(2,1)} %get-tuple-element.171., ...), custom_call_target="tpu_custom_call" | custom-call | flops 14495514624 | bytes 9437184 | tf_op jit(solution)/shard_map/pallas_call | solution.py:229
  443.0 56.1 %shard_map.86 = (bf16[384,768]{1,0:T(8,128)(2,1)}, bf16[384,768]{1,0:T(8,128)(2,1)}, bf16[384,768]{1,0:T(8,128)(2,1)}, bf16[384,768]{1,0:T(8,128)(2,1)}, bf16[38...) custom-call(bf16[384,768]{1,0:T(8,128)(2,1)} %get-tuple-element.203., ...), custom_call_target="tpu_custom_call" | custom-call | flops 14495514624 | bytes 9437184 | tf_op jit(solution)/shard_map/pallas_call | solution.py:229
  563.1 11.0 %collective-permute-done.100.refs_3_ = bf16[384,768]{1,0:T(8,128)(2,1)S(1)} collective-permute-done((bf16[384,768]{1,0:T(8,128)(2,1)}, bf16[384,768]{1,0:T(8,128)(2,1)S(1)}, u32[]{:S(2)}, u32[]{:S(2)}) %collective-permute-start.100) | collective-permute-done | bytes 589856 | tf_op jit(solution)/shard_map/ppermute | solution.py:347
  576.1 11.0 %collective-permute-done.103.refs_6_ = bf16[384,768]{1,0:T(8,128)(2,1)} collective-permute-done((bf16[384,768]{1,0:T(8,128)(2,1)}, bf16[384,768]{1,0:T(8,128)(2,1)}, u32[]{:S(2)}, u32[]{:S(2)}) %collective-permute-start.103) | collective-permute-done | bytes 589856 | tf_op jit(solution)/shard_map/ppermute | solution.py:347
  588.2 11.9 %collective-permute-done.104.refs_7_ = bf16[384,768]{1,0:T(8,128)(2,1)} collective-permute-done((bf16[384,768]{1,0:T(8,128)(2,1)}, bf16[384,768]{1,0:T(8,128)(2,1)}, u32[]{:S(2)}, u32[]{:S(2)}) %collective-permute-start.104) | collective-permute-done | bytes 589856 | tf_op jit(solution)/shard_map/ppermute | solution.py:347
  613.7 11.1 %collective-permute-done.79.refs_3_ = bf16[384,768]{1,0:T(8,128)(2,1)} collective-permute-done((bf16[384,768]{1,0:T(8,128)(2,1)}, bf16[384,768]{1,0:T(8,128)(2,1)}, u32[]{:S(2)}, u32[]{:S(2)}) %collective-permute-start.79) | collective-permute-done | bytes 589856 | tf_op jit(solution)/shard_map/ppermute | solution.py:347
  626.7 11.0 %collective-permute-done.82.refs_6_ = bf16[384,768]{1,0:T(8,128)(2,1)} collective-permute-done((bf16[384,768]{1,0:T(8,128)(2,1)}, bf16[384,768]{1,0:T(8,128)(2,1)}, u32[]{:S(2)}, u32[]{:S(2)}) %collective-permute-start.82) | collective-permute-done | bytes 589856 | tf_op jit(solution)/shard_map/ppermute | solution.py:347
  638.8 11.9 %collective-permute-done.83.refs_7_ = bf16[384,768]{1,0:T(8,128)(2,1)} collective-permute-done((bf16[384,768]{1,0:T(8,128)(2,1)}, bf16[384,768]{1,0:T(8,128)(2,1)}, u32[]{:S(2)}, u32[]{:S(2)}) %collective-permute-start.83) | collective-permute-done | bytes 589856 | tf_op jit(solution)/shard_map/ppermute | solution.py:347
  652.8 9.8 %collective-permute-done.64.refs_2_ = bf16[384,768]{1,0:T(8,128)(2,1)} collective-permute-done((bf16[384,768]{1,0:T(8,128)(2,1)}, bf16[384,768]{1,0:T(8,128)(2,1)}, u32[]{:S(2)}, u32[]{:S(2)}) %collective-permute-start.64) | collective-permute-done | bytes 589856 | tf_op jit(solution)/shard_map/ppermute | solution.py:347
  664.3 11.1 %collective-permute-done.65.refs_3_ = bf16[384,768]{1,0:T(8,128)(2,1)} collective-permute-done((bf16[384,768]{1,0:T(8,128)(2,1)}, bf16[384,768]{1,0:T(8,128)(2,1)}, u32[]{:S(2)}, u32[]{:S(2)}) %collective-permute-start.65) | collective-permute-done | bytes 589856 | tf_op jit(solution)/shard_map/ppermute | solution.py:347
  677.3 11.0 %collective-permute-done.68.refs_6_ = bf16[384,768]{1,0:T(8,128)(2,1)} collective-permute-done((bf16[384,768]{1,0:T(8,128)(2,1)}, bf16[384,768]{1,0:T(8,128)(2,1)}, u32[]{:S(2)}, u32[]{:S(2)}) %collective-permute-start.68) | collective-permute-done | bytes 589856 | tf_op jit(solution)/shard_map/ppermute | solution.py:347
  689.4 11.9 %collective-permute-done.69.refs_7_ = bf16[384,768]{1,0:T(8,128)(2,1)} collective-permute-done((bf16[384,768]{1,0:T(8,128)(2,1)}, bf16[384,768]{1,0:T(8,128)(2,1)}, u32[]{:S(2)}, u32[]{:S(2)}) %collective-permute-start.69) | collective-permute-done | bytes 589856 | tf_op jit(solution)/shard_map/ppermute | solution.py:347
  703.4 9.8 %collective-permute-done.50.refs_2_ = bf16[384,768]{1,0:T(8,128)(2,1)} collective-permute-done((bf16[384,768]{1,0:T(8,128)(2,1)}, bf16[384,768]{1,0:T(8,128)(2,1)}, u32[]{:S(2)}, u32[]{:S(2)}) %collective-permute-start.50) | collective-permute-done | bytes 589856 | tf_op jit(solution)/shard_map/ppermute | solution.py:347
  714.9 11.1 %collective-permute-done.51.refs_3_ = bf16[384,768]{1,0:T(8,128)(2,1)} collective-permute-done((bf16[384,768]{1,0:T(8,128)(2,1)}, bf16[384,768]{1,0:T(8,128)(2,1)}, u32[]{:S(2)}, u32[]{:S(2)}) %collective-permute-start.51) | collective-permute-done | bytes 589856 | tf_op jit(solution)/shard_map/ppermute | solution.py:347
  727.9 11.0 %collective-permute-done.54.refs_6_ = bf16[384,768]{1,0:T(8,128)(2,1)} collective-permute-done((bf16[384,768]{1,0:T(8,128)(2,1)}, bf16[384,768]{1,0:T(8,128)(2,1)}, u32[]{:S(2)}, u32[]{:S(2)}) %collective-permute-start.54) | collective-permute-done | bytes 589856 | tf_op jit(solution)/shard_map/ppermute | solution.py:347
  740.0 11.9 %collective-permute-done.55.refs_7_ = bf16[384,768]{1,0:T(8,128)(2,1)} collective-permute-done((bf16[384,768]{1,0:T(8,128)(2,1)}, bf16[384,768]{1,0:T(8,128)(2,1)}, u32[]{:S(2)}, u32[]{:S(2)}) %collective-permute-start.55) | collective-permute-done | bytes 589856 | tf_op jit(solution)/shard_map/ppermute | solution.py:347
  779.1 10.4 %collective-permute-done.40.refs_6_ = bf16[384,768]{1,0:T(8,128)(2,1)} collective-permute-done((bf16[384,768]{1,0:T(8,128)(2,1)}, bf16[384,768]{1,0:T(8,128)(2,1)}, u32[]{:S(2)}, u32[]{:S(2)}) %collective-permute-start.40) | collective-permute-done | bytes 589856 | tf_op jit(solution)/shard_map/ppermute | solution.py:347
  791.3 11.2 %collective-permute-done.41.refs_7_ = bf16[384,768]{1,0:T(8,128)(2,1)} collective-permute-done((bf16[384,768]{1,0:T(8,128)(2,1)}, bf16[384,768]{1,0:T(8,128)(2,1)}, u32[]{:S(2)}, u32[]{:S(2)}) %collective-permute-start.41) | collective-permute-done | bytes 589856 | tf_op jit(solution)/shard_map/ppermute | solution.py:347
  (339 shorter events, 287.9 us)
Async XLA Ops:
  74.6 65.5 %collective-permute-start.75 = (bf16[384,768]{1,0:T(8,128)(2,1)}, bf16[384,768]{1,0:T(8,128)(2,1)}, u32[]{:S(2)}, u32[]{:S(2)}) collective-permute-start(bf16[384,768]{1,0:T(8,128)(2,1)} %get-tuple-element.257), channel_id=1, source_target_pairs={{0,6},{1,7},{2,4},{3,5},{4,2},{5,3},{6,0},{7,1}} | collective-permute-start | bytes 1769480 | tf_op jit(solution)/shard_map/ppermute | solution.py:347
  76.4 64.8 %collective-permute-start.76 = (bf16[384,768]{1,0:T(8,128)(2,1)}, bf16[384,768]{1,0:T(8,128)(2,1)}, u32[]{:S(2)}, u32[]{:S(2)}) collective-permute-start(bf16[384,768]{1,0:T(8,128)(2,1)} %get-tuple-element.258), channel_id=1, source_target_pairs={{0,7},{1,6},{2,5},{3,4},{4,3},{5,2},{6,1},{7,0}} | collective-permute-start | bytes 1769480 | tf_op jit(solution)/shard_map/ppermute | solution.py:347
  140.0 60.1 %collective-permute-start.59 = (bf16[384,768]{1,0:T(8,128)(2,1)}, bf16[384,768]{1,0:T(8,128)(2,1)S(1)}, u32[]{:S(2)}, u32[]{:S(2)}) collective-permute-start(bf16[384,768]{1,0:T(8,128)(2,1)} %get-tuple-element.239), channel_id=1, source_target_pairs={{0,4},{1,5},{2,6},{3,7},{4,0},{5,1},{6,2},{7,3}} | collective-permute-start | bytes 1769480 | tf_op jit(solution)/shard_map/ppermute | solution.py:347
  141.2 60.0 %collective-permute-start.60 = (bf16[384,768]{1,0:T(8,128)(2,1)}, bf16[384,768]{1,0:T(8,128)(2,1)}, u32[]{:S(2)}, u32[]{:S(2)}) collective-permute-start(bf16[384,768]{1,0:T(8,128)(2,1)} %get-tuple-element.240), channel_id=1, source_target_pairs={{0,5},{1,4},{2,7},{3,6},{4,1},{5,0},{6,3},{7,2}} | collective-permute-start | bytes 1769480 | tf_op jit(solution)/shard_map/ppermute | solution.py:347
  141.2 60.8 %collective-permute-start.61 = (bf16[384,768]{1,0:T(8,128)(2,1)}, bf16[384,768]{1,0:T(8,128)(2,1)}, u32[]{:S(2)}, u32[]{:S(2)}) collective-permute-start(bf16[384,768]{1,0:T(8,128)(2,1)} %get-tuple-element.241), channel_id=1, source_target_pairs={{0,6},{1,7},{2,4},{3,5},{4,2},{5,3},{6,0},{7,1}} | collective-permute-start | bytes 1769480 | tf_op jit(solution)/shard_map/ppermute | solution.py:347
  142.5 60.7 %collective-permute-start.62 = (bf16[384,768]{1,0:T(8,128)(2,1)}, bf16[384,768]{1,0:T(8,128)(2,1)}, u32[]{:S(2)}, u32[]{:S(2)}) collective-permute-start(bf16[384,768]{1,0:T(8,128)(2,1)} %get-tuple-element.242), channel_id=1, source_target_pairs={{0,7},{1,6},{2,5},{3,4},{4,3},{5,2},{6,1},{7,0}} | collective-permute-start | bytes 1769480 | tf_op jit(solution)/shard_map/ppermute | solution.py:347
  144.5 59.2 %collective-permute-start.42 = (bf16[384,768]{1,0:T(8,128)(2,1)}, bf16[384,768]{1,0:T(8,128)(2,1)S(1)}, u32[]{:S(2)}, u32[]{:S(2)}) collective-permute-start(bf16[384,768]{1,0:T(8,128)(2,1)} %get-tuple-element.220), channel_id=1, source_target_pairs={{0,1},{1,0},{2,3},{3,2},{4,5},{5,4},{6,7},{7,6}} | collective-permute-start | bytes 1769480 | tf_op jit(solution)/shard_map/ppermute | solution.py:347
  200.2 61.3 %collective-permute-start.43 = (bf16[384,768]{1,0:T(8,128)(2,1)}, bf16[384,768]{1,0:T(8,128)(2,1)}, u32[]{:S(2)}, u32[]{:S(2)}) collective-permute-start(bf16[384,768]{1,0:T(8,128)(2,1)} %get-tuple-element.221), channel_id=1, source_target_pairs={{0,2},{1,3},{2,0},{3,1},{4,6},{5,7},{6,4},{7,5}} | collective-permute-start | bytes 1769480 | tf_op jit(solution)/shard_map/ppermute | solution.py:347
  201.2 61.2 %collective-permute-start.44 = (bf16[384,768]{1,0:T(8,128)(2,1)}, bf16[384,768]{1,0:T(8,128)(2,1)}, u32[]{:S(2)}, u32[]{:S(2)}) collective-permute-start(bf16[384,768]{1,0:T(8,128)(2,1)} %get-tuple-element.222), channel_id=1, source_target_pairs={{0,3},{1,2},{2,1},{3,0},{4,7},{5,6},{6,5},{7,4}} | collective-permute-start | bytes 1769480 | tf_op jit(solution)/shard_map/ppermute | solution.py:347
  202.0 60.7 %collective-permute-start.45 = (bf16[384,768]{1,0:T(8,128)(2,1)}, bf16[384,768]{1,0:T(8,128)(2,1)}, u32[]{:S(2)}, u32[]{:S(2)}) collective-permute-start(bf16[384,768]{1,0:T(8,128)(2,1)} %get-tuple-element.223), channel_id=1, source_target_pairs={{0,4},{1,5},{2,6},{3,7},{4,0},{5,1},{6,2},{7,3}} | collective-permute-start | bytes 1769480 | tf_op jit(solution)/shard_map/ppermute | solution.py:347
  203.2 60.6 %collective-permute-start.46 = (bf16[384,768]{1,0:T(8,128)(2,1)}, bf16[384,768]{1,0:T(8,128)(2,1)}, u32[]{:S(2)}, u32[]{:S(2)}) collective-permute-start(bf16[384,768]{1,0:T(8,128)(2,1)} %get-tuple-element.224), channel_id=1, source_target_pairs={{0,5},{1,4},{2,7},{3,6},{4,1},{5,0},{6,3},{7,2}} | collective-permute-start | bytes 1769480 | tf_op jit(solution)/shard_map/ppermute | solution.py:347
  203.7 60.1 %collective-permute-start.47 = (bf16[384,768]{1,0:T(8,128)(2,1)}, bf16[384,768]{1,0:T(8,128)(2,1)}, u32[]{:S(2)}, u32[]{:S(2)}) collective-permute-start(bf16[384,768]{1,0:T(8,128)(2,1)} %get-tuple-element.225), channel_id=1, source_target_pairs={{0,6},{1,7},{2,4},{3,5},{4,2},{5,3},{6,0},{7,1}} | collective-permute-start | bytes 1769480 | tf_op jit(solution)/shard_map/ppermute | solution.py:347
  262.7 59.9 %collective-permute-start.29 = (bf16[384,768]{1,0:T(8,128)(2,1)S(1)}, bf16[384,768]{1,0:T(8,128)(2,1)}, u32[]{:S(2)}, u32[]{:S(2)}) collective-permute-start(bf16[384,768]{1,0:T(8,128)(2,1)S(1)} %copy-done.38), channel_id=1, source_target_pairs={{0,2},{1,3},{2,0},{3,1},{4,6},{5,7},{6,4},{7,5}} | collective-permute-start | bytes 1769480 | tf_op jit(solution)/shard_map/ppermute | solution.py:347
  263.8 60.6 %collective-permute-start.1 = (bf16[384,768]{1,0:T(8,128)(2,1)S(1)}, bf16[384,768]{1,0:T(8,128)(2,1)}, u32[]{:S(2)}, u32[]{:S(2)}) collective-permute-start(bf16[384,768]{1,0:T(8,128)(2,1)S(1)} %copy-done.35), channel_id=1, source_target_pairs={{0,2},{1,3},{2,0},{3,1},{4,6},{5,7},{6,4},{7,5}} | collective-permute-start | bytes 1769480 | tf_op jit(solution)/shard_map/ppermute | solution.py:347
  320.4 61.3 %collective-permute-start.2 = (bf16[384,768]{1,0:T(8,128)(2,1)}, bf16[384,768]{1,0:T(8,128)(2,1)}, u32[]{:S(2)}, u32[]{:S(2)}) collective-permute-start(bf16[384,768]{1,0:T(8,128)(2,1)} %get-tuple-element.174), channel_id=1, source_target_pairs={{0,3},{1,2},{2,1},{3,0},{4,7},{5,6},{6,5},{7,4}} | collective-permute-start | bytes 1769480 | tf_op jit(solution)/shard_map/ppermute | solution.py:347
  321.3 61.3 %collective-permute-start.3 = (bf16[384,768]{1,0:T(8,128)(2,1)}, bf16[384,768]{1,0:T(8,128)(2,1)}, u32[]{:S(2)}, u32[]{:S(2)}) collective-permute-start(bf16[384,768]{1,0:T(8,128)(2,1)} %get-tuple-element.175), channel_id=1, source_target_pairs={{0,4},{1,5},{2,6},{3,7},{4,0},{5,1},{6,2},{7,3}} | collective-permute-start | bytes 1769480 | tf_op jit(solution)/shard_map/ppermute | solution.py:347
  322.6 61.1 %collective-permute-start.4 = (bf16[384,768]{1,0:T(8,128)(2,1)}, bf16[384,768]{1,0:T(8,128)(2,1)}, u32[]{:S(2)}, u32[]{:S(2)}) collective-permute-start(bf16[384,768]{1,0:T(8,128)(2,1)} %get-tuple-element.176), channel_id=1, source_target_pairs={{0,5},{1,4},{2,7},{3,6},{4,1},{5,0},{6,3},{7,2}} | collective-permute-start | bytes 1769480 | tf_op jit(solution)/shard_map/ppermute | solution.py:347
  323.0 61.2 %collective-permute-start.5 = (bf16[384,768]{1,0:T(8,128)(2,1)}, bf16[384,768]{1,0:T(8,128)(2,1)}, u32[]{:S(2)}, u32[]{:S(2)}) collective-permute-start(bf16[384,768]{1,0:T(8,128)(2,1)} %get-tuple-element.177), channel_id=1, source_target_pairs={{0,6},{1,7},{2,4},{3,5},{4,2},{5,3},{6,0},{7,1}} | collective-permute-start | bytes 1769480 | tf_op jit(solution)/shard_map/ppermute | solution.py:347
  324.5 61.5 %collective-permute-start.6 = (bf16[384,768]{1,0:T(8,128)(2,1)}, bf16[384,768]{1,0:T(8,128)(2,1)}, u32[]{:S(2)}, u32[]{:S(2)}) collective-permute-start(bf16[384,768]{1,0:T(8,128)(2,1)} %get-tuple-element.178), channel_id=1, source_target_pairs={{0,7},{1,6},{2,5},{3,4},{4,3},{5,2},{6,1},{7,0}} | collective-permute-start | bytes 1769480 | tf_op jit(solution)/shard_map/ppermute | solution.py:347
  381.7 60.9 %collective-permute-start.30 = (bf16[384,768]{1,0:T(8,128)(2,1)}, bf16[384,768]{1,0:T(8,128)(2,1)}, u32[]{:S(2)}, u32[]{:S(2)}) collective-permute-start(bf16[384,768]{1,0:T(8,128)(2,1)} %get-tuple-element.206), channel_id=1, source_target_pairs={{0,3},{1,2},{2,1},{3,0},{4,7},{5,6},{6,5},{7,4}} | collective-permute-start | bytes 1769480 | tf_op jit(solution)/shard_map/ppermute | solution.py:347
  382.6 60.2 %collective-permute-start.31 = (bf16[384,768]{1,0:T(8,128)(2,1)}, bf16[384,768]{1,0:T(8,128)(2,1)}, u32[]{:S(2)}, u32[]{:S(2)}) collective-permute-start(bf16[384,768]{1,0:T(8,128)(2,1)} %get-tuple-element.207), channel_id=1, source_target_pairs={{0,4},{1,5},{2,6},{3,7},{4,0},{5,1},{6,2},{7,3}} | collective-permute-start | bytes 1769480 | tf_op jit(solution)/shard_map/ppermute | solution.py:347
  442.6 68.6 %collective-permute-start.7 = (bf16[128,768]{1,0:T(8,128)(2,1)}, bf16[128,768]{1,0:T(8,128)(2,1)S(1)}, u32[]{:S(2)}, u32[]{:S(2)}) collective-permute-start(bf16[128,768]{1,0:T(8,128)(2,1)} %get-tuple-element.180), channel_id=1, source_target_pairs={{0,1},{1,0},{2,3},{3,2},{4,5},{5,4},{6,7},{7,6}} | collective-permute-start | bytes 589832 | tf_op jit(solution)/shard_map/ppermute | solution.py:347
  776.6 60.8 %collective-permute-start.9 = (bf16[128,768]{1,0:T(8,128)(2,1)}, bf16[128,768]{1,0:T(8,128)(2,1)S(1)}, u32[]{:S(2)}, u32[]{:S(2)}) collective-permute-start(bf16[128,768]{1,0:T(8,128)(2,1)} %get-tuple-element.182), channel_id=1, source_target_pairs={{0,3},{1,2},{2,1},{3,0},{4,7},{5,6},{6,5},{7,4}} | collective-permute-start | bytes 589832 | tf_op jit(solution)/shard_map/ppermute | solution.py:347
  777.4 60.0 %collective-permute-start.10 = (bf16[128,768]{1,0:T(8,128)(2,1)}, bf16[128,768]{1,0:T(8,128)(2,1)S(1)}, u32[]{:S(2)}, u32[]{:S(2)}) collective-permute-start(bf16[128,768]{1,0:T(8,128)(2,1)} %get-tuple-element.183), channel_id=1, source_target_pairs={{0,4},{1,5},{2,6},{3,7},{4,0},{5,1},{6,2},{7,3}} | collective-permute-start | bytes 589832 | tf_op jit(solution)/shard_map/ppermute | solution.py:347
  (146 other events, 7192.7 us)
